TPU v7x, 128 devices: a whole 4x4x4 slice. The times are simulated.
128 devices in a mesh: dp: 1, ing: 2 (over core), grp: 64 (over z, y, x).
Axes of the slice: x: 4, y: 4, z: 4, core: 2. Of those that a mesh axis runs over, the one named last changes fastest.
Arguments:
- x_first: bfloat16 [16384, 2048], P(('dp', 'grp', 'ing'))
- ids_first: int32 [16384, 8], P(('dp', 'grp', 'ing'))
- gates_first: float32 [16384, 8], P(('dp', 'grp', 'ing'))
- x_second: bfloat16 [16384, 2048], P(('dp', 'grp', 'ing'))
- ids_second: int32 [16384, 8], P(('dp', 'grp', 'ing'))
- gates_second: float32 [16384, 8], P(('dp', 'grp', 'ing'))
- w_one: bfloat16 [128, 2048, 768], P(('grp', 'ing'))
- w_three: bfloat16 [128, 2048, 768], P(('grp', 'ing'))
- w_two: bfloat16 [128, 768, 2048], P(('grp', 'ing'))
Outputs:
- output 1: bfloat16 [16384, 2048], P(('dp', 'grp', 'ing'))
- output 2: bfloat16 [16384, 2048], P(('dp', 'grp', 'ing'))
All inputs are finite; a program needn't handle non-finite values.
Results may differ from a plain program's by a relative error of at most 0.0108876.
Values are sent between devices in bfloat16 or wider.
A program may use at most 1 GiB of HBM per device.

v0:
```python
import functools

import jax
import jax.numpy as jnp
from jax import lax
from jax.experimental import pallas as pl
from jax.experimental.pallas import tpu as pltpu
from jax.sharding import PartitionSpec as P

MESH = pl.DeviceIdType.MESH
CAP = 8
LANES = 128


def lane_parts(hidden):
    tiles = hidden // LANES
    sizes = [(tiles // 3 + (1 if d < tiles % 3 else 0)) * LANES for d in range(3)]
    return [(sum(sizes[:d]), sizes[d]) for d in range(3)]


def moe_kernel(side, x1, x2, ids1, ids2, gt1, gt2, w1_hbm, w3_hbm, w2_hbm, y1, y2,
               ag, p2s, p2r, r2, zr, vt, vr, selt, fold, xr, gs, gr, w1, w3, w2, yacc,
               wsem, gsem, sems):
    xs, ys = (x1, x2), (y1, y2)
    tokens, hidden = x1.shape
    n = side ** 3 * 2
    plane = n // side
    rows = plane * CAP
    parts = lane_parts(hidden)
    grp = lax.axis_index('grp')
    ing = lax.axis_index('ing')
    me = (grp % side, (grp // side) % side, grp // (side * side))
    order = [(d, (d + 1) % 3, (d + 2) % 3) for d in range(3)]
    f32, bf16 = jnp.float32, jnp.bfloat16

    def at(off, core=0):
        x, y, z = ((m + o) % side for m, o in zip(me, off))
        return (z * side + y) * side + x, (ing + core) % 2

    def along(dim, step, core=0):
        off = [0, 0, 0]
        off[dim] = step % side
        return at(off, core)

    def remote(src, dst, send, recv, dev):
        return pltpu.make_async_remote_copy(src_ref=src, dst_ref=dst, send_sem=send, recv_sem=recv,
                                            device_id={'grp': dev[0], 'ing': dev[1]}, device_id_type=MESH)

    def iota(shape, dim):
        return lax.broadcasted_iota(jnp.int32, shape, dim)

    def split(q):
        return q // (side * side * 2), (q // (side * 2)) % side, (q // 2) % side, q % 2

    barrier = pltpu.get_barrier_semaphore()

    def knock(q, carry):
        ox, oy, oz, oc = split(q)
        dev = at((ox, oy, oz), oc)
        pl.semaphore_signal(barrier, inc=1, device_id={'grp': dev[0], 'ing': dev[1]}, device_id_type=MESH)
        return carry

    lax.fori_loop(1, n, knock, 0)
    weights = [pltpu.make_async_copy(src, dst, wsem.at[k])
               for k, (src, dst) in enumerate(((w1_hbm.at[0], w1), (w3_hbm.at[0], w3), (w2_hbm.at[0], w2)))]
    for copy in weights:
        copy.start()

    later = (iota((tokens, tokens), 0) < iota((tokens, tokens), 1)).astype(f32).astype(bf16)
    expert = iota((n, tokens), 0)
    gate_rows = jnp.zeros((n, LANES), f32)
    lane = iota((n, LANES), 1)
    for b, (ids, gates) in enumerate(((ids1, gt1), (ids2, gt2))):
        member = jnp.zeros((n, tokens), f32)
        gate = jnp.zeros((n, tokens), f32)
        for j in range(ids.shape[0]):
            hit = ids[j:j + 1, :] == expert
            member = jnp.where(hit, 1.0, member)
            gate = jnp.where(hit, gates[j:j + 1, :], gate)
        before = jnp.dot(member.astype(bf16), later, preferred_element_type=f32)
        table = jnp.where(member > 0.0, before + 1.0, 0.0)
        for d, (f, s, t) in enumerate(order):
            q = split(iota((n, n), 0))
            off = [None] * 3
            off[f], off[s], off[t] = q[0], q[1], q[2]
            to_grp, to_ing = at(off, q[3])
            perm = (to_grp * 2 + to_ing == iota((n, n), 1)).astype(f32).astype(bf16)
            vt[d][b] = jnp.dot(perm, table.astype(bf16), preferred_element_type=f32).astype(bf16)
            vr[d][b, 0] = vt[d][b, 0:plane, :]
        for k in range(CAP):
            col = jnp.sum(jnp.where(table == k + 1.0, gate, 0.0), axis=1, keepdims=True)
            gate_rows = jnp.where(lane == b * CAP + k, col, gate_rows)
    gs[...] = gate_rows[:, None, :]
    for b in range(2):
        for d, (lo, width) in enumerate(parts):
            ag[d][b, 0] = xs[b][:, lo:lo + width]

    def sem(phase, b, d, k):
        return sems[phase].at[0, b, d, k], sems[phase].at[1, b, d, k]

    def gather(b):
        out = []
        for i in range(1, side):
            for d, (f, s, t) in enumerate(order):
                lo, width = parts[d]
                dev = along(f, i)
                out.append(remote(vt[d].at[b, pl.ds(i * plane, plane)], vr[d].at[b, i], *sem(0, b, d, i), dev))
                out.append(remote(xs[b].at[:, pl.ds(lo, width)], ag[d].at[b, i], *sem(1, b, d, i), dev))
        return out

    def mid(d, b, j):
        f, s, t = order[d]
        return (b, slice(None), slice(None), slice(None), j) if f < s else (b, slice(None), slice(None), j)

    def second(b, steps):
        return [remote(p2s[d].at[b, j - 1], p2r[d].at[mid(d, b, j)], *sem(2, b, d, j), along(order[d][1], j))
                for j in steps for d in range(3)]

    def final(d, b, k, core):
        lo, width = parts[d]
        index = [slice(None)] * 3
        index[order[d][2]] = k
        return (b, *index, core, slice(None), pl.ds(lo, width))

    def third(b):
        return [remote(p2r[d].at[b, k, c], xr.at[final(d, b, k, c)], *sem(3, b, d, 2 * k + c), along(order[d][2], k, c))
                for k in range(side) for c in range(2) if k + c for d in range(3)]

    def back_third(b):
        return [remote(xr.at[final(d, b, k, c)], p2r[d].at[b, k, c], *sem(4, b, d, 2 * k + c),
                       along(order[d][2], -k, c))
                for k in range(side) for c in range(2) if k + c for d in range(3)]

    def back_second(b):
        return [remote(p2r[d].at[mid(d, b, j)], r2[d].at[b, j], *sem(5, b, d, j), along(order[d][1], -j))
                for j in range(1, side) for d in range(3)]

    def back_first(b, steps):
        return [remote(r2[d].at[b, :, :, :, i], zr[d].at[b, i], *sem(6, b, d, i), along(order[d][0], -i))
                for i in steps for d in range(3)]

    def start(copies):
        for copy in copies:
            copy.start()

    def arrived(copies):
        for copy in copies:
            copy.wait_recv()

    def left(copies):
        for copy in copies:
            copy.wait_send()

    def gate_copy(q):
        ox, oy, oz, oc = split(q)
        dev = at((ox, oy, oz), oc)
        return remote(gs.at[pl.ds(dev[0] * 2 + dev[1], 1)], gr.at[pl.ds(q, 1)], gsem.at[0], gsem.at[1], dev)

    def send_gate(q, carry):
        gate_copy(q).start()
        return carry

    gates_all = remote(gs.at[pl.ds(1, n - 1)], gr.at[pl.ds(1, n - 1)], gsem.at[0], gsem.at[1], (grp, ing))

    def expand():
        return (iota((rows, plane), 0) // CAP == iota((rows, plane), 1)).astype(f32).astype(bf16)

    def chosen(table):
        v = jnp.dot(expand(), table, preferred_element_type=f32)
        return jnp.where(v == (iota(v.shape, 0) % CAP + 1).astype(f32), 1.0, 0.0)

    def select(b):
        for d, (f, s, t) in enumerate(order):
            width = parts[d][1]

            def pick(i, carry, d=d, f=f, s=s, width=width):
                sel = chosen(vr[d][b, i]).astype(bf16)
                out = jnp.dot(sel, ag[d][b, i], preferred_element_type=f32)
                out = out.reshape(side, side, 2, CAP, width).astype(bf16)
                if f < s:
                    p2r[d][b, :, :, i, 0] = out[0]
                else:
                    p2r[d][b, :, :, 0, i] = out[0]
                for j in range(1, side):
                    p2s[d][b, j - 1, :, :, i] = out[j]
                return carry

            lax.fori_loop(0, side, pick, 0)

    def ffn(b, first, last):
        def chunk(ox, carry):
            rec = xr[b, ox].astype(f32).reshape(rows, hidden).astype(bf16)
            act_a = jnp.dot(rec, w1[...], preferred_element_type=f32)
            act_b = jnp.dot(rec, w3[...], preferred_element_type=f32)
            inner = (act_a * jax.nn.sigmoid(act_a) * act_b).astype(bf16)
            g = gr[pl.ds(ox * plane, plane)]
            g = jnp.broadcast_to(g, (plane, CAP, LANES)).reshape(rows, LANES)
            mine = iota(g.shape, 1) == b * CAP + iota(g.shape, 0) % CAP
            g = jnp.sum(jnp.where(mine, g, 0.0), axis=1, keepdims=True)
            out = jnp.dot(inner, w2[...], preferred_element_type=f32) * g
            xr[b, ox] = out.reshape(side, side, 2, CAP, hidden).astype(bf16)
            return carry

        lax.fori_loop(first, last, chunk, 0)

    def tables(b):
        for d in range(3):
            def one(i, carry, d=d):
                sel = chosen(vt[d][b, pl.ds(pl.multiple_of(i * plane, plane), plane), :])
                sel_t = sel.T.astype(bf16)
                same = jnp.dot(sel.astype(bf16), sel_t, preferred_element_type=f32)
                r, c = iota(same.shape, 0), iota(same.shape, 1)
                same = jnp.where(r // (2 * CAP) == c // (2 * CAP), same, 0.0)
                earlier = jnp.sum(jnp.where(c < r, same, 0.0), axis=1, keepdims=True)
                fold[d][i] = jnp.where(earlier > 0.0, 0.0, same).astype(bf16)
                selt[d][i] = sel_t
                return carry

            lax.fori_loop(0, side, one, 0)

    def combine(b):
        for d, (lo, width) in enumerate(parts):
            yacc[:, lo:lo + width] = jnp.zeros((tokens, width), f32)

            def one(i, carry, d=d, lo=lo, width=width):
                z = zr[d][b, i].astype(f32).reshape(rows, width).astype(bf16)
                part = jnp.dot(fold[d][i], z, preferred_element_type=f32).astype(bf16)
                yacc[:, lo:lo + width] += jnp.dot(selt[d][i], part, preferred_element_type=f32)
                return carry

            lax.fori_loop(0, side, one, 0)
        ys[b][...] = yacc[...].astype(bf16)

    def keep_third(b):
        for d in range(3):
            xr[final(d, b, 0, 0)] = p2r[d][b, 0, 0]

    def keep_back_third(b):
        for d in range(3):
            p2r[d][b, 0, 0] = xr[final(d, b, 0, 0)]

    def keep_back_second(b):
        for d in range(3):
            r2[d][b, 0] = p2r[d][mid(d, b, 0)]

    def keep_back_first(b):
        for d in range(3):
            zr[d][b, 0] = r2[d][b, :, :, :, 0]

    half = side // 2
    odd = [i for i in range(1, side) if i != half]

    pl.semaphore_wait(barrier, n - 1)
    start(gather(0))
    start(gather(1))
    lax.fori_loop(1, n, send_gate, 0)
    gr[0:1] = gs[pl.ds(grp * 2 + ing, 1)]

    arrived(gather(0))
    select(0)
    start(second(0, range(1, side)))
    arrived(gather(1))
    select(1)
    start(second(1, [half]))
    arrived(second(0, range(1, side)))
    start(third(0))
    start(second(1, odd))
    keep_third(0)
    for copy in weights:
        copy.wait()
    gates_all.wait_recv()
    arrived(third(0))
    ffn(0, 0, side - 1)
    arrived(second(1, range(1, side)))
    left(third(0))
    start(third(1))
    keep_third(1)
    ffn(0, side - 1, side)
    arrived(third(1))
    left(third(1))
    start(back_third(0))
    keep_back_third(0)
    ffn(1, 0, side - 1)
    arrived(back_third(0))
    start(back_second(0))
    keep_back_second(0)
    ffn(1, side - 1, side)
    start(back_third(1))
    keep_back_third(1)
    arrived(back_second(0))
    start(back_first(0, odd))
    keep_back_first(0)
    tables(0)
    arrived(back_third(1))
    start(back_second(1))
    keep_back_second(1)
    start(back_first(0, [half]))
    arrived(back_second(1))
    start(back_first(1, range(1, side)))
    keep_back_first(1)
    arrived(back_first(0, range(1, side)))
    combine(0)
    tables(1)
    arrived(back_first(1, range(1, side)))
    combine(1)

    gates_all.wait_send()
    for b in range(2):
        every = range(1, side)
        for copies in (gather(b), second(b, every), back_third(b), back_second(b), back_first(b, every)):
            left(copies)


def solution(mesh):
    n_grp = mesh.shape['grp']
    side = round(n_grp ** (1 / 3))
    n = side ** 3 * 2
    plane = n // side
    tok_spec = P(('dp', 'grp', 'ing'), None)
    w_spec = P(('grp', 'ing'), None, None)

    def body(x1, ids1, g1, x2, ids2, g2, w1, w3, w2):
        tokens, hidden = x1.shape
        ff = w1.shape[2]
        vmem = pl.BlockSpec(memory_space=pltpu.VMEM)
        hbm = pl.BlockSpec(memory_space=pl.ANY)
        out = jax.ShapeDtypeStruct((tokens, hidden), jnp.bfloat16)
        widths = [w for _, w in lane_parts(hidden)]

        def per_part(*shape):
            return [pltpu.VMEM((*shape, w), jnp.bfloat16) for w in widths]

        def per_dim(*shape):
            return [pltpu.VMEM(shape, jnp.bfloat16) for _ in widths]

        rows = plane * CAP
        gate = pltpu.VMEM((n, 1, LANES), jnp.float32)
        return pl.pallas_call(
            functools.partial(moe_kernel, side),
            out_shape=(out, out),
            in_specs=[vmem] * 6 + [hbm] * 3,
            out_specs=(vmem, vmem),
            scratch_shapes=[per_part(2, side, tokens),
                            per_part(2, side - 1, side, 2, side, CAP),
                            per_part(2, side, 2, side, side, CAP),
                            per_part(2, side, side, 2, side, CAP),
                            per_part(2, side, side, side, 2, CAP),
                            per_dim(2, n, tokens),
                            per_dim(2, side, plane, tokens),
                            per_dim(side, tokens, rows),
                            per_dim(side, rows, rows),
                            pltpu.VMEM((2, side, side, side, 2, CAP, hidden), jnp.bfloat16),
                            gate, gate,
                            pltpu.VMEM((hidden, ff), jnp.bfloat16),
                            pltpu.VMEM((hidden, ff), jnp.bfloat16),
                            pltpu.VMEM((ff, hidden), jnp.bfloat16),
                            pltpu.VMEM((tokens, hidden), jnp.float32),
                            pltpu.SemaphoreType.DMA((3,)), pltpu.SemaphoreType.DMA((2,)),
                            [pltpu.SemaphoreType.DMA((2, 2, 3, k * side)) for k in (1, 1, 1, 2, 2, 1, 1)]],
            compiler_params=pltpu.CompilerParams(collective_id=0, has_side_effects=True,
                                                 vmem_limit_bytes=67_000_000),
        )(x1, x2, ids1.T, ids2.T, g1.T, g2.T, w1, w3, w2)

    return jax.shard_map(body, mesh=mesh, in_specs=(tok_spec,) * 6 + (w_spec,) * 3,
                         out_specs=(tok_spec, tok_spec), check_vma=False)
```

profile of v0, /device:TPU:1, one launch (start us, length us, event | category | flops | bytes accessed | tf_op | source)
XLA Modules:
  0.0 214.2 jit_solution(1357715616562909850)
XLA Ops:
  0.6 209.8 %shard_map.104 = (bf16[128,2048]{1,0:T(8,128)(2,1)}, bf16[128,2048]{1,0:T(8,128)(2,1)}) custom-call(bf16[128,2048]{1,0:T(8,128)(2,1)} %x1.1, bf16[128,2048]{1,0:T(8,128)(2,1)} %x2.1, s32[8,128]{1,0:T(8,128)} %bitcast.4, s32[8,128]{1,0:T(8,128)} %bitcast.5, f32[8,128]{1,0:T(8,128)} %bitcast.6, f32[8,128]{1,0:T(8,128)} %bitcast.7, ...), custom_call_target="tpu_custom_call" | custom-call | tf_op jit(solution)/shard_map/pallas_call | solution.py:338
  210.5 1.9 copy.13
  212.3 1.9 copy.14
where the time goes:
time: 215 us; the launch traced here: 214 us
  Pallas kernels  210 us (98%)
  local copies, waits for them, and re-layouts  3.76 us (2%)
    pallas_call x1, Pallas kernels, body(): pl.pallas_call(functools.partial(moe_kernel, side), out_shape=(out, out),...  210 us

commit v1 on v0

v1 whole, which is shorter than its diff:
```python
import functools

import jax
import jax.numpy as jnp
from jax import lax
from jax.experimental import pallas as pl
from jax.experimental.pallas import tpu as pltpu
from jax.sharding import PartitionSpec as P

MESH = pl.DeviceIdType.MESH
CAP = 8
LANES = 128


def lane_parts(hidden):
    tiles = hidden // LANES
    sizes = [(tiles // 3 + (1 if d < tiles % 3 else 0)) * LANES for d in range(3)]
    return [(sum(sizes[:d]), sizes[d]) for d in range(3)]


def moe_kernel(side, x1, x2, ids1, ids2, gt1, gt2, w1_hbm, w3_hbm, w2_hbm, y1, y2,
               ag, p2s, p2r, r2, zr, vt, vr, selt, fold, xr, gs, gr, w1, w3, w2,
               wsem, gsem, sems):
    xs, ys = (x1, x2), (y1, y2)
    tokens, hidden = x1.shape
    n = side ** 3 * 2
    plane = n // side
    rows = plane * CAP
    parts = lane_parts(hidden)
    grp = lax.axis_index('grp')
    ing = lax.axis_index('ing')
    me = (grp % side, (grp // side) % side, grp // (side * side))
    order = [(d, (d + 1) % 3, (d + 2) % 3) for d in range(3)]
    f32, bf16 = jnp.float32, jnp.bfloat16

    def at(off, core=0):
        x, y, z = ((m + o) % side for m, o in zip(me, off))
        return (z * side + y) * side + x, (ing + core) % 2

    def along(dim, step, core=0):
        off = [0, 0, 0]
        off[dim] = step % side
        return at(off, core)

    def remote(src, dst, send, recv, dev):
        return pltpu.make_async_remote_copy(src_ref=src, dst_ref=dst, send_sem=send, recv_sem=recv,
                                            device_id={'grp': dev[0], 'ing': dev[1]}, device_id_type=MESH)

    def iota(shape, dim):
        return lax.broadcasted_iota(jnp.int32, shape, dim)

    def split(q):
        return q // (side * side * 2), (q // (side * 2)) % side, (q // 2) % side, q % 2

    barrier = pltpu.get_barrier_semaphore()
    for c in range(2):
        def knock(q, carry, c=c):
            pl.semaphore_signal(barrier, inc=1, device_id_type=MESH,
                                device_id={'grp': lax.rem(grp + q, n // 2), 'ing': lax.rem(ing + c, 2)})
            return carry

        lax.fori_loop(1 - c, n // 2, knock, 0)
    weights = [pltpu.make_async_copy(src, dst, wsem.at[k])
               for k, (src, dst) in enumerate(((w1_hbm.at[0], w1), (w3_hbm.at[0], w3), (w2_hbm.at[0], w2)))]
    for copy in weights:
        copy.start()

    def expert_at(q, d):
        off = [None] * 3
        for dim, o in zip(order[d], split(q)):
            off[dim] = o
        to_grp, to_ing = at(off, q % 2)
        return to_grp * 2 + to_ing

    later = (iota((tokens, tokens), 0) < iota((tokens, tokens), 1)).astype(f32).astype(bf16)
    expert = expert_at(iota((n, 1), 0), 0)
    gate_rows = jnp.zeros((n, LANES), f32)
    lane = iota((n, LANES), 1)
    perms = [(expert_at(iota((n, 1), 0), d) == expert_at(iota((1, n), 1), 0)).astype(f32).astype(bf16) for d in (1, 2)]
    for b, (ids, gates) in enumerate(((ids1, gt1), (ids2, gt2))):
        member = jnp.zeros((n, tokens), f32)
        gate = jnp.zeros((n, tokens), f32)
        for j in range(ids.shape[0]):
            hit = ids[j:j + 1, :] == expert
            member = jnp.where(hit, 1.0, member)
            gate = jnp.where(hit, gates[j:j + 1, :], gate)
        before = jnp.dot(member.astype(bf16), later, preferred_element_type=f32)
        table = jnp.where(member > 0.0, before + 1.0, 0.0)
        short = table.astype(bf16)
        for d in range(3):
            vt[d][b] = jnp.dot(perms[d - 1], short, preferred_element_type=f32).astype(bf16) if d else short
            vr[d][b, 0] = vt[d][b, 0:plane, :]
        for k in range(CAP):
            col = jnp.sum(jnp.where(table == k + 1.0, gate, 0.0), axis=1, keepdims=True)
            gate_rows = jnp.where(lane == b * CAP + k, col, gate_rows)
    gs[...] = gate_rows[:, None, :]
    for b in range(2):
        for d, (lo, width) in enumerate(parts):
            ag[d][b, 0] = xs[b][:, lo:lo + width]

    up = [f < s for f, s, t in order]
    every = range(1, side)
    ends = [(k, c) for k in range(side) for c in range(2) if k + c]

    def sem(phase, b, d, k):
        return sems[phase].at[0, b, d, k], sems[phase].at[1, b, d, k]

    def gather(b, d):
        lo, width = parts[d]
        out = []
        for i in every:
            dev = along(order[d][0], i)
            out.append(remote(vt[d].at[b, pl.ds(i * plane, plane)], vr[d].at[b, i], *sem(0, b, d, i), dev))
            out.append(remote(xs[b].at[:, pl.ds(lo, width)], ag[d].at[b, i], *sem(1, b, d, i), dev))
        return out

    def mid(d, b, j):
        return (b, slice(None), slice(None), slice(None), j) if up[d] else (b, slice(None), slice(None), j)

    def second(b, d):
        return [remote(p2s[d].at[b, j], p2r[d].at[mid(d, b, j)], *sem(2, b, d, j), along(order[d][1], j)) for j in every]

    def final(d, b, k, core):
        lo, width = parts[d]
        index = [slice(None)] * 3
        index[order[d][2]] = k
        return (b, *index, core, slice(None), pl.ds(lo, width))

    def third(b, d):
        return [remote(p2r[d].at[b, k, c], xr.at[final(d, b, k, c)], *sem(3, b, d, 2 * k + c), along(order[d][2], k, c))
                for k, c in ends]

    def back_third(b, d):
        return [remote(xr.at[final(d, b, k, c)], p2s[d].at[b, :, k, c], *sem(4, b, d, 2 * k + c),
                       along(order[d][2], -k, c)) for k, c in ends]

    def back_mid(d, b, j):
        return (b, slice(None), slice(None), slice(None), j) if up[d] else (b, j)

    def back_second(b, d):
        return [remote(p2s[d].at[back_mid(d, b, j)], r2[d].at[b, j], *sem(5, b, d, j), along(order[d][1], -j))
                for j in every]

    def back_near(d, b, i):
        return (b, slice(None), i) if up[d] else (b, slice(None), slice(None), slice(None), i)

    def back_first(b, d):
        return [remote(r2[d].at[back_near(d, b, i)], zr[d].at[b, i], *sem(6, b, d, i), along(order[d][0], -i))
                for i in every]

    def gate_copy(q):
        ox, oy, oz, oc = split(q)
        return remote(gs.at[pl.ds(q, 1)], gr.at[pl.ds(q, 1)], gsem.at[0], gsem.at[1], at((ox, oy, oz), oc))

    def send_gate(q, carry):
        gate_copy(q).start()
        return carry

    gates_all = remote(gs.at[pl.ds(1, n - 1)], gr.at[pl.ds(1, n - 1)], gsem.at[0], gsem.at[1], (grp, ing))

    def start(copies):
        for copy in copies:
            copy.start()

    def arrived(copies):
        for copy in copies:
            copy.wait_recv()

    def left(copies):
        for copy in copies:
            copy.wait_send()

    def expand():
        return (iota((rows, plane), 0) // CAP == iota((rows, plane), 1)).astype(f32).astype(bf16)

    def chosen(table):
        v = jnp.dot(expand(), table, preferred_element_type=f32)
        return jnp.where(v == (iota(v.shape, 0) % CAP + 1).astype(f32), 1.0, 0.0)

    def select(b, d):
        width = parts[d][1]

        def pick(i, carry):
            sel = chosen(vr[d][b, i]).astype(bf16)
            out = jnp.dot(sel, ag[d][b, i], preferred_element_type=f32)
            out = out.reshape(side, side, 2, CAP, width).astype(bf16)
            if up[d]:
                p2r[d][b, :, :, i, 0] = out[0]
            else:
                p2r[d][b, :, :, 0, i] = out[0]
            for j in every:
                p2s[d][b, j, :, :, i] = out[j]
            return carry

        lax.fori_loop(0, side, pick, 0)

    def ffn(b):
        def chunk(ox, carry):
            rec = xr[b, ox].astype(f32).reshape(rows, hidden).astype(bf16)
            act_a = jnp.dot(rec, w1[...], preferred_element_type=f32)
            act_b = jnp.dot(rec, w3[...], preferred_element_type=f32)
            inner = (act_a * jax.nn.sigmoid(act_a) * act_b).astype(bf16)
            g = gr[pl.ds(ox * plane, plane)]
            g = jnp.broadcast_to(g, (plane, CAP, LANES)).reshape(rows, LANES)
            mine = iota(g.shape, 1) == b * CAP + iota(g.shape, 0) % CAP
            g = jnp.sum(jnp.where(mine, g, 0.0), axis=1, keepdims=True)
            out = jnp.dot(inner, w2[...], preferred_element_type=f32) * g
            xr[b, ox] = out.reshape(side, side, 2, CAP, hidden).astype(bf16)
            return carry

        lax.fori_loop(0, side, chunk, 0)

    def tables(b):
        for d in range(3):
            def one(i, carry, d=d):
                sel = chosen(vt[d][b, pl.ds(pl.multiple_of(i * plane, plane), plane), :])
                sel_t = sel.T.astype(bf16)
                same = jnp.dot(sel.astype(bf16), sel_t, preferred_element_type=f32)
                r, c = iota(same.shape, 0), iota(same.shape, 1)
                same = jnp.where(r // (2 * CAP) == c // (2 * CAP), same, 0.0)
                earlier = jnp.sum(jnp.where(c < r, same, 0.0), axis=1, keepdims=True)
                fold[d][i] = jnp.where(earlier > 0.0, 0.0, same).astype(bf16)
                selt[d][i] = sel_t
                return carry

            lax.fori_loop(0, side, one, 0)

    def combine(b, d):
        lo, width = parts[d]
        ys[b][:, lo:lo + width] = jnp.zeros((tokens, width), f32)

        def one(i, carry):
            z = zr[d][b, i].astype(f32).reshape(rows, width).astype(bf16)
            part = jnp.dot(fold[d][i], z, preferred_element_type=f32).astype(bf16)
            ys[b][:, lo:lo + width] += jnp.dot(selt[d][i], part, preferred_element_type=f32)
            return carry

        lax.fori_loop(0, side, one, 0)

    narrow_first = (1, 2, 0)
    pl.semaphore_wait(barrier, n - 1)
    for b in range(2):
        for d in narrow_first:
            start(gather(b, d))
    lax.fori_loop(1, n, send_gate, 0)
    gr[0:1] = gs[0:1]
    for b in range(2):
        for d in narrow_first:
            arrived(gather(b, d))
            select(b, d)
            start(second(b, d))
    for b in range(2):
        for d in narrow_first:
            arrived(second(b, d))
            left(second(b, d))
            start(third(b, d))
            xr[final(d, b, 0, 0)] = p2r[d][b, 0, 0]
    for copy in weights:
        copy.wait()
    for b in range(2):
        for d in narrow_first:
            arrived(third(b, d))
        if b == 0:
            gates_all.wait_recv()
        ffn(b)
        for d in narrow_first:
            start(back_third(b, d))
            p2s[d][b, :, 0, 0] = xr[final(d, b, 0, 0)]
    for b in range(2):
        for d in narrow_first:
            arrived(back_third(b, d))
            start(back_second(b, d))
            r2[d][b, 0] = p2s[d][back_mid(d, b, 0)]
    for b in range(2):
        for d in narrow_first:
            arrived(back_second(b, d))
            start(back_first(b, d))
            zr[d][b, 0] = r2[d][back_near(d, b, 0)]
        if b == 0:
            tables(0)
    for b in range(2):
        for d in narrow_first:
            arrived(back_first(b, d))
            combine(b, d)
        if b == 0:
            tables(1)

    gates_all.wait_send()
    for b in range(2):
        for d in range(3):
            left(gather(b, d) + third(b, d) + back_third(b, d) + back_second(b, d) + back_first(b, d))


def solution(mesh):
    n_grp = mesh.shape['grp']
    side = round(n_grp ** (1 / 3))
    n = side ** 3 * 2
    plane = n // side
    tok_spec = P(('dp', 'grp', 'ing'), None)
    w_spec = P(('grp', 'ing'), None, None)

    def body(x1, ids1, g1, x2, ids2, g2, w1, w3, w2):
        tokens, hidden = x1.shape
        ff = w1.shape[2]
        vmem = pl.BlockSpec(memory_space=pltpu.VMEM)
        hbm = pl.BlockSpec(memory_space=pl.ANY)
        out = jax.ShapeDtypeStruct((tokens, hidden), jnp.float32)
        widths = [w for _, w in lane_parts(hidden)]

        def per_part(*shape):
            return [pltpu.VMEM((*shape, w), jnp.bfloat16) for w in widths]

        def per_dim(*shape):
            return [pltpu.VMEM(shape, jnp.bfloat16) for _ in widths]

        rows = plane * CAP
        gate = pltpu.VMEM((n, 1, LANES), jnp.float32)
        y1, y2 = pl.pallas_call(
            functools.partial(moe_kernel, side),
            out_shape=(out, out),
            in_specs=[vmem] * 6 + [hbm] * 3,
            out_specs=(vmem, vmem),
            scratch_shapes=[per_part(2, side, tokens),
                            per_part(2, side, side, 2, side, CAP),
                            per_part(2, side, 2, side, side, CAP),
                            [pltpu.VMEM((2, side, *((side, side, 2) if d < 2 else (side, 2, side)), CAP, w), jnp.bfloat16)
                             for d, w in enumerate(widths)],
                            per_part(2, side, side, side, 2, CAP),
                            per_dim(2, n, tokens),
                            per_dim(2, side, plane, tokens),
                            per_dim(side, tokens, rows),
                            per_dim(side, rows, rows),
                            pltpu.VMEM((2, side, side, side, 2, CAP, hidden), jnp.bfloat16),
                            gate, gate,
                            pltpu.VMEM((hidden, ff), jnp.bfloat16),
                            pltpu.VMEM((hidden, ff), jnp.bfloat16),
                            pltpu.VMEM((ff, hidden), jnp.bfloat16),
                            pltpu.SemaphoreType.DMA((3,)), pltpu.SemaphoreType.DMA((2,)),
                            [pltpu.SemaphoreType.DMA((2, 2, 3, k * side)) for k in (1, 1, 1, 2, 2, 1, 1)]],
            compiler_params=pltpu.CompilerParams(collective_id=0, has_side_effects=True,
                                                 vmem_limit_bytes=67_000_000),
        )(x1, x2, ids1.T, ids2.T, g1.T, g2.T, w1, w3, w2)
        return y1.astype(jnp.bfloat16), y2.astype(jnp.bfloat16)

    return jax.shard_map(body, mesh=mesh, in_specs=(tok_spec,) * 6 + (w_spec,) * 3,
                         out_specs=(tok_spec, tok_spec), check_vma=False)
```

time: 215 us -> 201 us (0.935)
  Pallas kernels: 210 us -> 194 us
  other arithmetic: 0 us -> 4.17 us
  local copies, waits for them, and re-layouts: 3.76 us -> 0 us
    pallas_call x1, Pallas kernels: 210 us -> 194 us  [body(): pl.pallas_call(functools.partial(moe_kernel, side), out_shape=(out, out),...]
    convert_element_type x0 -> x2, other arithmetic: none -> 4.17 us  [body(): return (y1.astype(jnp.bfloat16), y2.astype(jnp.bfloat16))]
    unnamed x2 -> x0, local copies, waits for them, and re-layouts: 3.76 us -> none
where the time goes in v1:
time: 201 us; the launch traced here: 198 us
  Pallas kernels  194 us (97%)
  other arithmetic  4.17 us (2%)
    pallas_call x1, Pallas kernels, body(): pl.pallas_call(functools.partial(moe_kernel, side), out_shape=(out, out),...  194 us
    convert_element_type x2, other arithmetic, body(): return (y1.astype(jnp.bfloat16), y2.astype(jnp.bfloat16))  4.17 us

profile of v1, /device:TPU:1, one launch (start us, length us, event | category | flops | bytes accessed | tf_op | source)
XLA Modules:
  0.0 198.5 jit_solution(2157535663622153918)
XLA Ops:
  0.6 193.7 %shard_map.104 = (f32[128,2048]{1,0:T(8,128)}, f32[128,2048]{1,0:T(8,128)}) custom-call(bf16[128,2048]{1,0:T(8,128)(2,1)} %x1.1, bf16[128,2048]{1,0:T(8,128)(2,1)} %x2.1, s32[8,128]{1,0:T(8,128)} %bitcast.4, s32[8,128]{1,0:T(8,128)} %bitcast.5, f32[8,128]{1,0:T(8,128)} %bitcast.6, f32[8,128]{1,0:T(8,128)} %bitcast.7, bf16[1,2048,768]{2,1,0:T(8,128)(2,1)} %w1_hbm.1, ...), custom_call_target="tpu_custom_call" | custom-call | tf_op jit(solution)/shard_map/pallas_call | solution.py:318
  194.3 2.1 %convert_element_type.6 = bf16[128,2048]{1,0:T(8,128)(2,1)} convert(f32[128,2048]{1,0:T(8,128)} %get-tuple-element.4) | non-fusion elementwise | flops 262144 | bytes 1572864 | tf_op jit(solution)/shard_map/convert_element_type | solution.py:343
  196.4 2.1 %convert_element_type.7 = bf16[128,2048]{1,0:T(8,128)(2,1)} convert(f32[128,2048]{1,0:T(8,128)} %get-tuple-element.5) | non-fusion elementwise | flops 262144 | bytes 1572864 | tf_op jit(solution)/shard_map/convert_element_type | solution.py:343

commit v2 on v1

--- a/solution.py
+++ b/solution.py
@@ -18,10 +18,10 @@
     return [(sum(sizes[:d]), sizes[d]) for d in range(3)]
 
 
-def moe_kernel(side, x1, x2, ids1, ids2, gt1, gt2, w1_hbm, w3_hbm, w2_hbm, y1, y2,
-               ag, p2s, p2r, r2, zr, vt, vr, selt, fold, xr, gs, gr, w1, w3, w2,
+def moe_kernel(side, x1, x2, ids1, ids2, gt1, gt2, w1_hbm, w3_hbm, w2_hbm, y,
+               ag, p2s, p2r, r2, zr, vt, vr, selt, fold, xr, gs, ga, gb, gr, w1, w3, w2, yacc,
                wsem, gsem, sems):
-    xs, ys = (x1, x2), (y1, y2)
+    xs = (x1, x2)
     tokens, hidden = x1.shape
     n = side ** 3 * 2
     plane = n // side
@@ -53,13 +53,14 @@
         return q // (side * side * 2), (q // (side * 2)) % side, (q // 2) % side, q % 2
 
     barrier = pltpu.get_barrier_semaphore()
-    for c in range(2):
-        def knock(q, carry, c=c):
-            pl.semaphore_signal(barrier, inc=1, device_id_type=MESH,
-                                device_id={'grp': lax.rem(grp + q, n // 2), 'ing': lax.rem(ing + c, 2)})
+    for dim in range(3):
+        def knock(q, carry, dim=dim):
+            dev = along(dim, q // 2, q % 2)
+            pl.semaphore_signal(barrier, inc=1, device_id={'grp': dev[0], 'ing': dev[1]}, device_id_type=MESH)
             return carry
 
-        lax.fori_loop(1 - c, n // 2, knock, 0)
+        lax.fori_loop(2 if dim else 1, 2 * side, knock, 0)
+    peers = 6 * side - 5
     weights = [pltpu.make_async_copy(src, dst, wsem.at[k])
                for k, (src, dst) in enumerate(((w1_hbm.at[0], w1), (w3_hbm.at[0], w3), (w2_hbm.at[0], w2)))]
     for copy in weights:
@@ -106,12 +107,11 @@
         return sems[phase].at[0, b, d, k], sems[phase].at[1, b, d, k]
 
     def gather(b, d):
-        lo, width = parts[d]
         out = []
         for i in every:
             dev = along(order[d][0], i)
             out.append(remote(vt[d].at[b, pl.ds(i * plane, plane)], vr[d].at[b, i], *sem(0, b, d, i), dev))
-            out.append(remote(xs[b].at[:, pl.ds(lo, width)], ag[d].at[b, i], *sem(1, b, d, i), dev))
+            out.append(remote(ag[d].at[b, 0], ag[d].at[b, i], *sem(1, b, d, i), dev))
         return out
 
     def mid(d, b, j):
@@ -148,15 +148,19 @@
         return [remote(r2[d].at[back_near(d, b, i)], zr[d].at[b, i], *sem(6, b, d, i), along(order[d][0], -i))
                 for i in every]
 
-    def gate_copy(q):
-        ox, oy, oz, oc = split(q)
-        return remote(gs.at[pl.ds(q, 1)], gr.at[pl.ds(q, 1)], gsem.at[0], gsem.at[1], at((ox, oy, oz), oc))
-
-    def send_gate(q, carry):
-        gate_copy(q).start()
-        return carry
-
-    gates_all = remote(gs.at[pl.ds(1, n - 1)], gr.at[pl.ds(1, n - 1)], gsem.at[0], gsem.at[1], (grp, ing))
+    far = 2 * side
+
+    def gate_first():
+        return [remote(gs.at[pl.ds(i * plane, plane)], ga.at[i], gsem.at[0, 0, i], gsem.at[1, 0, i], along(0, i))
+                for i in every]
+
+    def gate_second():
+        return [remote(ga.at[:, pl.ds(j * far, far)], gb.at[:, j], gsem.at[0, 1, j], gsem.at[1, 1, j], along(1, j))
+                for j in every]
+
+    def gate_third():
+        return [remote(gb.at[:, :, 2 * k + c], gr.at[:, :, 2 * k + c], gsem.at[0, 2, 2 * k + c],
+                       gsem.at[1, 2, 2 * k + c], along(2, k, c)) for k, c in ends]
 
     def start(copies):
         for copy in copies:
@@ -165,6 +169,9 @@
     def arrived(copies):
         for copy in copies:
             copy.wait_recv()
+
+    def mixed(lists):
+        return [copy for turn in zip(*lists) for copy in turn]
 
     def left(copies):
         for copy in copies:
@@ -200,7 +207,7 @@
             act_a = jnp.dot(rec, w1[...], preferred_element_type=f32)
             act_b = jnp.dot(rec, w3[...], preferred_element_type=f32)
             inner = (act_a * jax.nn.sigmoid(act_a) * act_b).astype(bf16)
-            g = gr[pl.ds(ox * plane, plane)]
+            g = gr[ox].reshape(plane, 1, LANES)
             g = jnp.broadcast_to(g, (plane, CAP, LANES)).reshape(rows, LANES)
             mine = iota(g.shape, 1) == b * CAP + iota(g.shape, 0) % CAP
             g = jnp.sum(jnp.where(mine, g, 0.0), axis=1, keepdims=True)
@@ -227,68 +234,131 @@
 
     def combine(b, d):
         lo, width = parts[d]
-        ys[b][:, lo:lo + width] = jnp.zeros((tokens, width), f32)
+        yacc[:, lo:lo + width] = jnp.zeros((tokens, width), f32)
 
         def one(i, carry):
             z = zr[d][b, i].astype(f32).reshape(rows, width).astype(bf16)
             part = jnp.dot(fold[d][i], z, preferred_element_type=f32).astype(bf16)
-            ys[b][:, lo:lo + width] += jnp.dot(selt[d][i], part, preferred_element_type=f32)
+            yacc[:, lo:lo + width] += jnp.dot(selt[d][i], part, preferred_element_type=f32)
             return carry
 
         lax.fori_loop(0, side, one, 0)
+        y[b, :, lo:lo + width] = yacc[:, lo:lo + width].astype(bf16)
 
     narrow_first = (1, 2, 0)
-    pl.semaphore_wait(barrier, n - 1)
-    for b in range(2):
-        for d in narrow_first:
-            start(gather(b, d))
-    lax.fori_loop(1, n, send_gate, 0)
-    gr[0:1] = gs[0:1]
-    for b in range(2):
+
+    def both(body):
+        def step(b, carry):
+            body(b)
+            return carry
+
+        lax.fori_loop(0, 2, step, 0)
+
+    def gather_tokens(b):
+        start(mixed([gather(b, d) for d in narrow_first]))
+        pl.when(b == 0)(lambda: start(gate_first()))
+
+    def pick_rows(b):
         for d in narrow_first:
             arrived(gather(b, d))
             select(b, d)
             start(second(b, d))
-    for b in range(2):
+
+        @pl.when(b == 0)
+        def _():
+            arrived(gate_first())
+            start(gate_second())
+            gb[:, 0] = ga[:, 0:far]
+
+    def last_hop(b):
         for d in narrow_first:
             arrived(second(b, d))
             left(second(b, d))
             start(third(b, d))
             xr[final(d, b, 0, 0)] = p2r[d][b, 0, 0]
-    for copy in weights:
-        copy.wait()
-    for b in range(2):
+
+        @pl.when(b == 0)
+        def _():
+            arrived(gate_second())
+            start(gate_third())
+            gr[:, :, 0] = gb[:, :, 0]
+
+    def experts(b):
         for d in narrow_first:
             arrived(third(b, d))
-        if b == 0:
-            gates_all.wait_recv()
+        pl.when(b == 0)(lambda: arrived(gate_third()))
         ffn(b)
-        for d in narrow_first:
-            start(back_third(b, d))
+        start(mixed([back_third(b, d) for d in narrow_first]))
+        for d in narrow_first:
             p2s[d][b, :, 0, 0] = xr[final(d, b, 0, 0)]
-    for b in range(2):
+
+    def return_second(b):
         for d in narrow_first:
             arrived(back_third(b, d))
             start(back_second(b, d))
             r2[d][b, 0] = p2s[d][back_mid(d, b, 0)]
-    for b in range(2):
+
+    def return_first(b):
         for d in narrow_first:
             arrived(back_second(b, d))
             start(back_first(b, d))
             zr[d][b, 0] = r2[d][back_near(d, b, 0)]
-        if b == 0:
-            tables(0)
-    for b in range(2):
+
+    def finish(b):
         for d in narrow_first:
             arrived(back_first(b, d))
             combine(b, d)
-        if b == 0:
-            tables(1)
-
-    gates_all.wait_send()
-    for b in range(2):
+        pl.when(b == 0)(lambda: tables(1))
+
+    def drain(b):
         for d in range(3):
             left(gather(b, d) + third(b, d) + back_third(b, d) + back_second(b, d) + back_first(b, d))
+
+    pl.semaphore_wait(barrier, peers)
+    ga[0] = gs[0:plane]
+    both(gather_tokens)
+    both(pick_rows)
+    both(last_hop)
+    for copy in weights:
+        copy.wait()
+    both(experts)
+    both(return_second)
+    both(return_first)
+    tables(0)
+    both(finish)
+    left(gate_first() + gate_second() + gate_third())
+    both(drain)
+
+
+def copy_kernel(y, y1, y2, buf, sem):
+    pieces = buf.shape[0] // 2
+    size = buf.shape[1]
+    moves = []
+    for k in range(pieces):
+        for b, dst in enumerate((y1, y2)):
+            slot = 2 * k + b
+            part = pl.ds(k * size, size)
+            moves.append((pltpu.make_async_copy(y.at[b, part], buf.at[slot], sem.at[0, slot]),
+                          pltpu.make_async_copy(buf.at[slot], dst.at[part], sem.at[1, slot])))
+    for come, _ in moves:
+        come.start()
+    for come, go in moves:
+        come.wait()
+        go.start()
+    for _, go in moves:
+        go.wait()
+
+
+def hand_on(y, pieces=4):
+    hbm = pl.BlockSpec(memory_space=pl.ANY)
+    _, tokens, hidden = y.shape
+    shape = jax.ShapeDtypeStruct((tokens, hidden), y.dtype)
+    if tokens // pieces % 16:
+        pieces = 1
+    return pl.pallas_call(
+        copy_kernel, out_shape=(shape, shape), in_specs=[hbm], out_specs=(hbm, hbm),
+        scratch_shapes=[pltpu.VMEM((2 * pieces, tokens // pieces, hidden), y.dtype),
+                        pltpu.SemaphoreType.DMA((2, 2 * pieces))])(y)
 
 
 def solution(mesh):
@@ -304,7 +374,7 @@
         ff = w1.shape[2]
         vmem = pl.BlockSpec(memory_space=pltpu.VMEM)
         hbm = pl.BlockSpec(memory_space=pl.ANY)
-        out = jax.ShapeDtypeStruct((tokens, hidden), jnp.float32)
+        out = jax.ShapeDtypeStruct((2, tokens, hidden), jnp.bfloat16)
         widths = [w for _, w in lane_parts(hidden)]
 
         def per_part(*shape):
@@ -314,12 +384,15 @@
             return [pltpu.VMEM(shape, jnp.bfloat16) for _ in widths]
 
         rows = plane * CAP
-        gate = pltpu.VMEM((n, 1, LANES), jnp.float32)
-        y1, y2 = pl.pallas_call(
+
+        def gate(*shape):
+            return pltpu.VMEM((*shape, 1, LANES), jnp.float32)
+
+        y = pl.pallas_call(
             functools.partial(moe_kernel, side),
-            out_shape=(out, out),
+            out_shape=out,
             in_specs=[vmem] * 6 + [hbm] * 3,
-            out_specs=(vmem, vmem),
+            out_specs=vmem,
             scratch_shapes=[per_part(2, side, tokens),
                             per_part(2, side, side, 2, side, CAP),
                             per_part(2, side, 2, side, side, CAP),
@@ -331,16 +404,17 @@
                             per_dim(side, tokens, rows),
                             per_dim(side, rows, rows),
                             pltpu.VMEM((2, side, side, side, 2, CAP, hidden), jnp.bfloat16),
-                            gate, gate,
+                            gate(n), gate(side, plane), gate(side, side, 2 * side), gate(side, side, 2 * side),
                             pltpu.VMEM((hidden, ff), jnp.bfloat16),
                             pltpu.VMEM((hidden, ff), jnp.bfloat16),
                             pltpu.VMEM((ff, hidden), jnp.bfloat16),
-                            pltpu.SemaphoreType.DMA((3,)), pltpu.SemaphoreType.DMA((2,)),
+                            pltpu.VMEM((tokens, hidden), jnp.float32),
+                            pltpu.SemaphoreType.DMA((3,)), pltpu.SemaphoreType.DMA((2, 3, 2 * side)),
                             [pltpu.SemaphoreType.DMA((2, 2, 3, k * side)) for k in (1, 1, 1, 2, 2, 1, 1)]],
             compiler_params=pltpu.CompilerParams(collective_id=0, has_side_effects=True,
                                                  vmem_limit_bytes=67_000_000),
         )(x1, x2, ids1.T, ids2.T, g1.T, g2.T, w1, w3, w2)
-        return y1.astype(jnp.bfloat16), y2.astype(jnp.bfloat16)
+        return hand_on(y)
 
     return jax.shard_map(body, mesh=mesh, in_specs=(tok_spec,) * 6 + (w_spec,) * 3,
                          out_specs=(tok_spec, tok_spec), check_vma=False)

time: 201 us -> 197 us (0.980); the launches traced: 198 us -> 197 us
  other arithmetic: 4.17 us -> 0 us
    convert_element_type x2 -> x0, other arithmetic: 4.17 us -> none  [body(): return (y1.astype(jnp.bfloat16), y2.astype(jnp.bfloat16))]
    pallas_call x1 -> x2, Pallas kernels: 194 us -> 196 us  [the longest x1 194 us: body(): pl.pallas_call(functools.partial(moe_kernel, side), out_shape=out, in_spe...]
where the time goes in v2:
time: 197 us
  Pallas kernels  196 us (99%)
    pallas_call x1, Pallas kernels, body(): pl.pallas_call(functools.partial(moe_kernel, side), out_shape=out, in_spe...  194 us

profile of v2, /device:TPU:1, one launch (start us, length us, event | category | flops | bytes accessed | tf_op | source)
XLA Modules:
  0.0 197.1 jit_solution(11305231138919165918)
XLA Ops:
  0.6 194.3 %shard_map.104.y = bf16[2,128,2048]{2,1,0:T(8,128)(2,1)} custom-call(bf16[128,2048]{1,0:T(8,128)(2,1)} %x1.1, bf16[128,2048]{1,0:T(8,128)(2,1)} %x2.1, s32[8,128]{1,0:T(8,128)} %bitcast.4, s32[8,128]{1,0:T(8,128)} %bitcast.5, f32[8,128]{1,0:T(8,128)} %bitcast.6, f32[8,128]{1,0:T(8,128)} %bitcast.7, bf16[1,2048,768]{2,1,0:T(8,128)(2,1)} %w1_hbm.1, ...), custom_call_target="tpu_custom_call" | custom-call | tf_op jit(solution)/shard_map/pallas_call | solution.py:391
  195.0 2.1 %shard_map.105 = (bf16[128,2048]{1,0:T(8,128)(2,1)}, bf16[128,2048]{1,0:T(8,128)(2,1)}) custom-call(bf16[2,128,2048]{2,1,0:T(8,128)(2,1)} %shard_map.104.y), custom_call_target="tpu_custom_call" | custom-call | tf_op jit(solution)/shard_map/pallas_call | solution.py:358

commit v3 on v2

--- a/solution.py
+++ b/solution.py
@@ -19,7 +19,7 @@
 
 
 def moe_kernel(side, x1, x2, ids1, ids2, gt1, gt2, w1_hbm, w3_hbm, w2_hbm, y,
-               ag, p2s, p2r, r2, zr, vt, vr, selt, fold, xr, gs, ga, gb, gr, w1, w3, w2, yacc,
+               ag, p2s, p2r, r2, ps, pr, rel, vt, vr, xr, gs, ga, gb, gr, w1, w3, w2,
                wsem, gsem, sems):
     xs = (x1, x2)
     tokens, hidden = x1.shape
@@ -144,9 +144,27 @@
     def back_near(d, b, i):
         return (b, slice(None), i) if up[d] else (b, slice(None), slice(None), slice(None), i)
 
+    low, high = pl.ds(0, tokens // 2), pl.ds(tokens // 2, tokens // 2)
+    ring = side > 2
+
+    def back_relay(b, d):
+        f = order[d][0]
+        return [remote(ps[d].at[b, 1, low], rel[d].at[b, 0], *sem(6, b, d, 0), along(f, -1)),
+                remote(ps[d].at[b, 1, high], rel[d].at[b, 1], *sem(6, b, d, 1), along(f, 1))] if ring else []
+
     def back_first(b, d):
-        return [remote(r2[d].at[back_near(d, b, i)], zr[d].at[b, i], *sem(6, b, d, i), along(order[d][0], -i))
-                for i in every]
+        f = order[d][0]
+        out = [remote(ps[d].at[b, 0, high], pr[d].at[b, 0, high], *sem(6, b, d, 2), along(f, -1))]
+        if ring:
+            out.append(remote(ps[d].at[b, 2, low], pr[d].at[b, 1, low], *sem(6, b, d, 3), along(f, 1)))
+        return out
+
+    def back_last(b, d):
+        f = order[d][0]
+        out = [remote(ps[d].at[b, 0, low], pr[d].at[b, 0, low], *sem(6, b, d, 4), along(f, -1))]
+        if ring:
+            out.append(remote(ps[d].at[b, 2, high], pr[d].at[b, 1, high], *sem(6, b, d, 5), along(f, 1)))
+        return out
 
     far = 2 * side
 
@@ -220,30 +238,26 @@
     def tables(b):
         for d in range(3):
             def one(i, carry, d=d):
-                sel = chosen(vt[d][b, pl.ds(pl.multiple_of(i * plane, plane), plane), :])
+                sel = chosen(vr[d][b, i])
                 sel_t = sel.T.astype(bf16)
                 same = jnp.dot(sel.astype(bf16), sel_t, preferred_element_type=f32)
                 r, c = iota(same.shape, 0), iota(same.shape, 1)
                 same = jnp.where(r // (2 * CAP) == c // (2 * CAP), same, 0.0)
                 earlier = jnp.sum(jnp.where(c < r, same, 0.0), axis=1, keepdims=True)
-                fold[d][i] = jnp.where(earlier > 0.0, 0.0, same).astype(bf16)
-                selt[d][i] = sel_t
+                fold = jnp.where(earlier > 0.0, 0.0, same).astype(bf16)
+                for k in range(rows // tokens):
+                    ag[d][0, i, :, k * rows:(k + 1) * rows] = fold[k * tokens:(k + 1) * tokens]
+                ag[d][1, i, :, 0:rows] = sel_t
                 return carry
 
             lax.fori_loop(0, side, one, 0)
 
-    def combine(b, d):
-        lo, width = parts[d]
-        yacc[:, lo:lo + width] = jnp.zeros((tokens, width), f32)
-
-        def one(i, carry):
-            z = zr[d][b, i].astype(f32).reshape(rows, width).astype(bf16)
-            part = jnp.dot(fold[d][i], z, preferred_element_type=f32).astype(bf16)
-            yacc[:, lo:lo + width] += jnp.dot(selt[d][i], part, preferred_element_type=f32)
-            return carry
-
-        lax.fori_loop(0, side, one, 0)
-        y[b, :, lo:lo + width] = yacc[:, lo:lo + width].astype(bf16)
+    def partial(b, d, i):
+        width = parts[d][1]
+        z = r2[d][back_near(d, b, i)].astype(f32).reshape(rows, width).astype(bf16)
+        fold = jnp.concatenate([ag[d][0, i, :, k * rows:(k + 1) * rows] for k in range(rows // tokens)], axis=0)
+        part = jnp.dot(fold, z, preferred_element_type=f32).astype(bf16)
+        return jnp.dot(ag[d][1, i, :, 0:rows], part, preferred_element_type=f32)
 
     narrow_first = (1, 2, 0)
 
@@ -299,20 +313,37 @@
             r2[d][b, 0] = p2s[d][back_mid(d, b, 0)]
 
     def return_first(b):
-        for d in narrow_first:
+        for d, (lo, width) in [(d, parts[d]) for d in narrow_first]:
             arrived(back_second(b, d))
-            start(back_first(b, d))
-            zr[d][b, 0] = r2[d][back_near(d, b, 0)]
+
+            def one(i, carry, d=d):
+                ps[d][b, i - 1] = partial(b, d, i)
+                return carry
+
+            lax.fori_loop(1, side, one, 0)
+            start(back_relay(b, d) + back_first(b, d))
+            y[b, :, lo:lo + width] = partial(b, d, 0)
+        pl.when(b == 0)(lambda: tables(1))
+
+    def pass_on(b):
+        half = tokens // 2
+        for d in narrow_first:
+            arrived(back_relay(b, d))
+            if ring:
+                ps[d][b, 0, 0:half] += rel[d][b, 0]
+                ps[d][b, 2, half:tokens] += rel[d][b, 1]
+            start(back_last(b, d))
 
     def finish(b):
-        for d in narrow_first:
-            arrived(back_first(b, d))
-            combine(b, d)
-        pl.when(b == 0)(lambda: tables(1))
+        for d, (lo, width) in [(d, parts[d]) for d in narrow_first]:
+            arrived(back_first(b, d) + back_last(b, d))
+            total = y[b, :, lo:lo + width] + pr[d][b, 0]
+            y[b, :, lo:lo + width] = total + pr[d][b, 1] if ring else total
 
     def drain(b):
         for d in range(3):
-            left(gather(b, d) + third(b, d) + back_third(b, d) + back_second(b, d) + back_first(b, d))
+            left(third(b, d) + back_third(b, d) + back_second(b, d))
+            left(back_relay(b, d) + back_first(b, d) + back_last(b, d))
 
     pl.semaphore_wait(barrier, peers)
     ga[0] = gs[0:plane]
@@ -322,15 +353,17 @@
     for copy in weights:
         copy.wait()
     both(experts)
+    both(lambda b: [left(gather(b, d)) for d in range(3)])
+    tables(0)
     both(return_second)
     both(return_first)
-    tables(0)
+    both(pass_on)
     both(finish)
     left(gate_first() + gate_second() + gate_third())
     both(drain)
 
 
-def copy_kernel(y, y1, y2, buf, sem):
+def copy_kernel(y, y1, y2, buf, narrow, sem):
     pieces = buf.shape[0] // 2
     size = buf.shape[1]
     moves = []
@@ -339,11 +372,12 @@
             slot = 2 * k + b
             part = pl.ds(k * size, size)
             moves.append((pltpu.make_async_copy(y.at[b, part], buf.at[slot], sem.at[0, slot]),
-                          pltpu.make_async_copy(buf.at[slot], dst.at[part], sem.at[1, slot])))
+                          pltpu.make_async_copy(narrow.at[slot], dst.at[part], sem.at[1, slot])))
     for come, _ in moves:
         come.start()
-    for come, go in moves:
+    for slot, (come, go) in enumerate(moves):
         come.wait()
+        narrow[slot] = buf[slot].astype(narrow.dtype)
         go.start()
     for _, go in moves:
         go.wait()
@@ -352,12 +386,13 @@
 def hand_on(y, pieces=4):
     hbm = pl.BlockSpec(memory_space=pl.ANY)
     _, tokens, hidden = y.shape
-    shape = jax.ShapeDtypeStruct((tokens, hidden), y.dtype)
+    shape = jax.ShapeDtypeStruct((tokens, hidden), jnp.bfloat16)
     if tokens // pieces % 16:
         pieces = 1
     return pl.pallas_call(
         copy_kernel, out_shape=(shape, shape), in_specs=[hbm], out_specs=(hbm, hbm),
         scratch_shapes=[pltpu.VMEM((2 * pieces, tokens // pieces, hidden), y.dtype),
+                        pltpu.VMEM((2 * pieces, tokens // pieces, hidden), jnp.bfloat16),
                         pltpu.SemaphoreType.DMA((2, 2 * pieces))])(y)
 
 
@@ -374,11 +409,14 @@
         ff = w1.shape[2]
         vmem = pl.BlockSpec(memory_space=pltpu.VMEM)
         hbm = pl.BlockSpec(memory_space=pl.ANY)
-        out = jax.ShapeDtypeStruct((2, tokens, hidden), jnp.bfloat16)
+        out = jax.ShapeDtypeStruct((2, tokens, hidden), jnp.float32)
         widths = [w for _, w in lane_parts(hidden)]
 
         def per_part(*shape):
             return [pltpu.VMEM((*shape, w), jnp.bfloat16) for w in widths]
+
+        def wide(*shape):
+            return [pltpu.VMEM((*shape, w), jnp.float32) for w in widths]
 
         def per_dim(*shape):
             return [pltpu.VMEM(shape, jnp.bfloat16) for _ in widths]
@@ -398,19 +436,16 @@
                             per_part(2, side, 2, side, side, CAP),
                             [pltpu.VMEM((2, side, *((side, side, 2) if d < 2 else (side, 2, side)), CAP, w), jnp.bfloat16)
                              for d, w in enumerate(widths)],
-                            per_part(2, side, side, side, 2, CAP),
+                            wide(2, side - 1, tokens), wide(2, 2, tokens), wide(2, 2, tokens // 2),
                             per_dim(2, n, tokens),
                             per_dim(2, side, plane, tokens),
-                            per_dim(side, tokens, rows),
-                            per_dim(side, rows, rows),
                             pltpu.VMEM((2, side, side, side, 2, CAP, hidden), jnp.bfloat16),
                             gate(n), gate(side, plane), gate(side, side, 2 * side), gate(side, side, 2 * side),
                             pltpu.VMEM((hidden, ff), jnp.bfloat16),
                             pltpu.VMEM((hidden, ff), jnp.bfloat16),
                             pltpu.VMEM((ff, hidden), jnp.bfloat16),
-                            pltpu.VMEM((tokens, hidden), jnp.float32),
                             pltpu.SemaphoreType.DMA((3,)), pltpu.SemaphoreType.DMA((2, 3, 2 * side)),
-                            [pltpu.SemaphoreType.DMA((2, 2, 3, k * side)) for k in (1, 1, 1, 2, 2, 1, 1)]],
+                            [pltpu.SemaphoreType.DMA((2, 2, 3, k * side)) for k in (1, 1, 1, 2, 2, 1, 3)]],
             compiler_params=pltpu.CompilerParams(collective_id=0, has_side_effects=True,
                                                  vmem_limit_bytes=67_000_000),
         )(x1, x2, ids1.T, ids2.T, g1.T, g2.T, w1, w3, w2)

time: 197 us -> 185 us (0.939)
  Pallas kernels: 196 us -> 184 us
    pallas_call x1, Pallas kernels: 194 us -> 182 us  [body(): pl.pallas_call(functools.partial(moe_kernel, side), out_shape=out, in_spe...]
where the time goes in v3:
time: 185 us
  Pallas kernels  184 us (99%)
    pallas_call x1, Pallas kernels, body(): pl.pallas_call(functools.partial(moe_kernel, side), out_shape=out, in_spe...  182 us

profile of v3, /device:TPU:1, one launch (start us, length us, event | category | flops | bytes accessed | tf_op | source)
XLA Modules:
  0.0 184.7 jit_solution(5739198393248466531)
XLA Ops:
  0.6 181.8 %shard_map.104.y = f32[2,128,2048]{2,1,0:T(8,128)} custom-call(bf16[128,2048]{1,0:T(8,128)(2,1)} %x1.1, bf16[128,2048]{1,0:T(8,128)(2,1)} %x2.1, s32[8,128]{1,0:T(8,128)} %bitcast.4, s32[8,128]{1,0:T(8,128)} %bitcast.5, f32[8,128]{1,0:T(8,128)} %bitcast.6, f32[8,128]{1,0:T(8,128)} %bitcast.7, bf16[1,2048,768]{2,1,0:T(8,128)(2,1)} %w1_hbm.1, ...), custom_call_target="tpu_custom_call" | custom-call | tf_op jit(solution)/shard_map/pallas_call | solution.py:429
  182.4 2.3 %shard_map.105 = (bf16[128,2048]{1,0:T(8,128)(2,1)}, bf16[128,2048]{1,0:T(8,128)(2,1)}) custom-call(f32[2,128,2048]{2,1,0:T(8,128)} %shard_map.104.y), custom_call_target="tpu_custom_call" | custom-call | tf_op jit(solution)/shard_map/pallas_call | solution.py:392

commit v4 on v3

v4 whole, which is shorter than its diff:
```python
import functools

import jax
import jax.numpy as jnp
from jax import lax
from jax.experimental import pallas as pl
from jax.experimental.pallas import tpu as pltpu
from jax.sharding import PartitionSpec as P

MESH = pl.DeviceIdType.MESH
CAP = 8
LANES = 128


def lane_parts(hidden):
    tiles = hidden // LANES
    sizes = [(tiles // 3 + (1 if d < tiles % 3 else 0)) * LANES for d in range(3)]
    return [(sum(sizes[:d]), sizes[d]) for d in range(3)]


def moe_kernel(side, x1, x2, ids1, ids2, gt1, gt2, w1_hbm, w3_hbm, w2_hbm, y,
               ag, p2s, p2r, r2, ps, pr, rel, vt, vr, xr, gs, ga, gb, gr, w1, w3, w2, total, rounded,
               xsem, ysem, wsem, gsem, sems):
    xs = (x1, x2)
    tokens, hidden = x1.shape
    n = side ** 3 * 2
    plane = n // side
    rows = plane * CAP
    parts = lane_parts(hidden)
    grp = lax.axis_index('grp')
    ing = lax.axis_index('ing')
    me = (grp % side, (grp // side) % side, grp // (side * side))
    order = [(d, (d + 1) % 3, (d + 2) % 3) for d in range(3)]
    f32, bf16 = jnp.float32, jnp.bfloat16

    def at(off, core=0):
        x, y, z = ((m + o) % side for m, o in zip(me, off))
        return (z * side + y) * side + x, (ing + core) % 2

    def along(dim, step, core=0):
        off = [0, 0, 0]
        off[dim] = step % side
        return at(off, core)

    def remote(src, dst, send, recv, dev):
        return pltpu.make_async_remote_copy(src_ref=src, dst_ref=dst, send_sem=send, recv_sem=recv,
                                            device_id={'grp': dev[0], 'ing': dev[1]}, device_id_type=MESH)

    def iota(shape, dim):
        return lax.broadcasted_iota(jnp.int32, shape, dim)

    def split(q):
        return q // (side * side * 2), (q // (side * 2)) % side, (q // 2) % side, q % 2

    barrier = pltpu.get_barrier_semaphore()
    for dim in range(3):
        def knock(q, carry, dim=dim):
            dev = along(dim, q // 2, q % 2)
            pl.semaphore_signal(barrier, inc=1, device_id={'grp': dev[0], 'ing': dev[1]}, device_id_type=MESH)
            return carry

        lax.fori_loop(2 if dim else 1, 2 * side, knock, 0)
    peers = 6 * side - 5
    own = [[pltpu.make_async_copy(xs[b].at[:, pl.ds(lo, width)], ag[d].at[b, 0], xsem.at[b, d])
            for d, (lo, width) in enumerate(parts)] for b in range(2)]
    for copy in own[0] + own[1]:
        copy.start()
    def expert_at(q, d):
        off = [None] * 3
        for dim, o in zip(order[d], split(q)):
            off[dim] = o
        to_grp, to_ing = at(off, q % 2)
        return to_grp * 2 + to_ing

    up = [f < s for f, s, t in order]
    every = range(1, side)
    ends = [(k, c) for k in range(side) for c in range(2) if k + c]

    def sem(phase, b, d, k):
        return sems[phase].at[0, b, d, k], sems[phase].at[1, b, d, k]

    low, high = pl.ds(0, tokens // 2), pl.ds(tokens // 2, tokens // 2)
    ring = side > 2

    def gather_tables(b, d):
        return [remote(vt[d].at[b, pl.ds(i * plane, plane)], vr[d].at[b, i], *sem(0, b, d, i), along(order[d][0], i))
                for i in every]

    def gather_near(b, d):
        f = order[d][0]
        return [remote(ag[d].at[b, 0], ag[d].at[b, i], *sem(1, b, d, i), along(f, i)) for i in ((1, side - 1) if ring else (1,))]

    def gather_relay(b, d):
        f = order[d][0]
        return [remote(ag[d].at[b, 1, low], ag[d].at[b, 2, low], *sem(1, b, d, 2), along(f, 1)),
                remote(ag[d].at[b, side - 1, high], ag[d].at[b, 2, high], *sem(1, b, d, 0), along(f, -1))] if ring else []

    def mid(d, b, j):
        return (b, slice(None), slice(None), slice(None), j) if up[d] else (b, slice(None), slice(None), j)

    def second(b, d):
        return [remote(p2s[d].at[b, j], p2r[d].at[mid(d, b, j)], *sem(2, b, d, j), along(order[d][1], j)) for j in every]

    def final(d, b, k, core):
        lo, width = parts[d]
        index = [slice(None)] * 3
        index[order[d][2]] = k
        return (b, *index, core, slice(None), pl.ds(lo, width))

    def third(b, d):
        return [remote(p2r[d].at[b, k, c], xr.at[final(d, b, k, c)], *sem(3, b, d, 2 * k + c), along(order[d][2], k, c))
                for k, c in ends]

    def back_third(b, d):
        return [remote(xr.at[final(d, b, k, c)], p2s[d].at[b, :, k, c], *sem(4, b, d, 2 * k + c),
                       along(order[d][2], -k, c)) for k, c in ends]

    def back_mid(d, b, j):
        return (b, slice(None), slice(None), slice(None), j) if up[d] else (b, j)

    def back_second(b, d):
        return [remote(p2s[d].at[back_mid(d, b, j)], r2[d].at[b, j], *sem(5, b, d, j), along(order[d][1], -j))
                for j in every]

    def back_near(d, b, i):
        return (b, slice(None), i) if up[d] else (b, slice(None), slice(None), slice(None), i)

    def back_relay(b, d):
        f = order[d][0]
        return [remote(ps[d].at[b, 1, low], rel[d].at[b, 0], *sem(6, b, d, 0), along(f, -1)),
                remote(ps[d].at[b, 1, high], rel[d].at[b, 1], *sem(6, b, d, 1), along(f, 1))] if ring else []

    def back_first(b, d):
        f = order[d][0]
        out = [remote(ps[d].at[b, 0, high], pr[d].at[b, 0, high], *sem(6, b, d, 2), along(f, -1))]
        if ring:
            out.append(remote(ps[d].at[b, 2, low], pr[d].at[b, 1, low], *sem(6, b, d, 3), along(f, 1)))
        return out

    def back_last(b, d):
        f = order[d][0]
        out = [remote(ps[d].at[b, 0, low], pr[d].at[b, 0, low], *sem(6, b, d, 4), along(f, -1))]
        if ring:
            out.append(remote(ps[d].at[b, 2, high], pr[d].at[b, 1, high], *sem(6, b, d, 5), along(f, 1)))
        return out

    far = 2 * side

    def gate_first():
        return [remote(gs.at[pl.ds(i * plane, plane)], ga.at[i], gsem.at[0, 0, i], gsem.at[1, 0, i], along(0, i))
                for i in every]

    def gate_second():
        return [remote(ga.at[:, pl.ds(j * far, far)], gb.at[:, j], gsem.at[0, 1, j], gsem.at[1, 1, j], along(1, j))
                for j in every]

    def gate_third():
        return [remote(gb.at[:, :, 2 * k + c], gr.at[:, :, 2 * k + c], gsem.at[0, 2, 2 * k + c],
                       gsem.at[1, 2, 2 * k + c], along(2, k, c)) for k, c in ends]

    def start(copies):
        for copy in copies:
            copy.start()

    def arrived(copies):
        for copy in copies:
            copy.wait_recv()

    def mixed(lists):
        return [copy for turn in zip(*lists) for copy in turn]

    def left(copies):
        for copy in copies:
            copy.wait_send()

    def expand():
        return (iota((rows, plane), 0) // CAP == iota((rows, plane), 1)).astype(f32).astype(bf16)

    def chosen(table):
        v = jnp.dot(expand(), table, preferred_element_type=f32)
        return jnp.where(v == (iota(v.shape, 0) % CAP + 1).astype(f32), 1.0, 0.0)

    def select(b, d):
        width = parts[d][1]

        def pick(i, carry):
            sel = chosen(vr[d][b, i]).astype(bf16)
            out = jnp.dot(sel, ag[d][b, i], preferred_element_type=f32)
            out = out.reshape(side, side, 2, CAP, width).astype(bf16)
            if up[d]:
                p2r[d][b, :, :, i, 0] = out[0]
            else:
                p2r[d][b, :, :, 0, i] = out[0]
            for j in every:
                p2s[d][b, j, :, :, i] = out[j]
            return carry

        lax.fori_loop(0, side, pick, 0)

    def ffn(b):
        def chunk(ox, carry):
            rec = xr[b, ox].astype(f32).reshape(rows, hidden).astype(bf16)
            act_a = jnp.dot(rec, w1[...], preferred_element_type=f32)
            act_b = jnp.dot(rec, w3[...], preferred_element_type=f32)
            inner = (act_a * jax.nn.sigmoid(act_a) * act_b).astype(bf16)
            g = gr[ox].reshape(plane, 1, LANES)
            g = jnp.broadcast_to(g, (plane, CAP, LANES)).reshape(rows, LANES)
            mine = iota(g.shape, 1) == b * CAP + iota(g.shape, 0) % CAP
            g = jnp.sum(jnp.where(mine, g, 0.0), axis=1, keepdims=True)
            out = jnp.dot(inner, w2[...], preferred_element_type=f32) * g
            xr[b, ox] = out.reshape(side, side, 2, CAP, hidden).astype(bf16)
            return carry

        lax.fori_loop(0, side, chunk, 0)

    def tables(b):
        for d in range(3):
            def one(i, carry, d=d):
                sel = chosen(vr[d][b, i])
                sel_t = sel.T.astype(bf16)
                same = jnp.dot(sel.astype(bf16), sel_t, preferred_element_type=f32)
                r, c = iota(same.shape, 0), iota(same.shape, 1)
                same = jnp.where(r // (2 * CAP) == c // (2 * CAP), same, 0.0)
                earlier = jnp.sum(jnp.where(c < r, same, 0.0), axis=1, keepdims=True)
                fold = jnp.where(earlier > 0.0, 0.0, same).astype(bf16)
                for k in range(rows // tokens):
                    ag[d][0, i, :, k * rows:(k + 1) * rows] = fold[k * tokens:(k + 1) * tokens]
                ag[d][1, i, :, 0:rows] = sel_t
                return carry

            lax.fori_loop(0, side, one, 0)

    def partial(b, d, i):
        width = parts[d][1]
        z = r2[d][back_near(d, b, i)].astype(f32).reshape(rows, width).astype(bf16)
        fold = jnp.concatenate([ag[d][0, i, :, k * rows:(k + 1) * rows] for k in range(rows // tokens)], axis=0)
        part = jnp.dot(fold, z, preferred_element_type=f32).astype(bf16)
        return jnp.dot(ag[d][1, i, :, 0:rows], part, preferred_element_type=f32)

    narrow_first = (1, 2, 0)

    def both(body):
        def step(b, carry):
            body(b)
            return carry

        lax.fori_loop(0, 2, step, 0)

    def gather_rest(b):
        for d in narrow_first:
            arrived(gather_near(b, d))
            start(gather_relay(b, d))

    def pick_rows(b):
        for d in narrow_first:
            arrived(gather_tables(b, d) + gather_relay(b, d))
            select(b, d)
            start(second(b, d))

        @pl.when(b == 0)
        def _():
            arrived(gate_first())
            start(gate_second())
            gb[:, 0] = ga[:, 0:far]

    def last_hop(b):
        for d in narrow_first:
            arrived(second(b, d))
            left(second(b, d))
            start(third(b, d))
            xr[final(d, b, 0, 0)] = p2r[d][b, 0, 0]

        @pl.when(b == 0)
        def _():
            arrived(gate_second())
            start(gate_third())
            gr[:, :, 0] = gb[:, :, 0]

    def experts(b):
        for d in narrow_first:
            arrived(third(b, d))
        pl.when(b == 0)(lambda: arrived(gate_third()))
        ffn(b)
        start(mixed([back_third(b, d) for d in narrow_first]))
        for d in narrow_first:
            p2s[d][b, :, 0, 0] = xr[final(d, b, 0, 0)]

    def return_second(b):
        for d in narrow_first:
            arrived(back_third(b, d))
            start(back_second(b, d))
            r2[d][b, 0] = p2s[d][back_mid(d, b, 0)]

    def return_first(b):
        for d, (lo, width) in [(d, parts[d]) for d in narrow_first]:
            arrived(back_second(b, d))

            def one(i, carry, d=d):
                ps[d][b, i - 1] = partial(b, d, i)
                return carry

            lax.fori_loop(1, side, one, 0)
            start(back_relay(b, d) + back_first(b, d))
            total[b, :, lo:lo + width] = partial(b, d, 0)
        pl.when(b == 0)(lambda: tables(1))

    def pass_on(b):
        half = tokens // 2
        for d in narrow_first:
            arrived(back_relay(b, d))
            if ring:
                ps[d][b, 0, 0:half] += rel[d][b, 0]
                ps[d][b, 2, half:tokens] += rel[d][b, 1]
            start(back_last(b, d))

    def result(b):
        return pltpu.make_async_copy(rounded.at[b], y.at[b], ysem.at[b])

    def finish(b):
        for d, (lo, width) in [(d, parts[d]) for d in narrow_first]:
            arrived(back_first(b, d) + back_last(b, d))
            out = total[b, :, lo:lo + width] + pr[d][b, 0]
            out = out + pr[d][b, 1] if ring else out
            rounded[b, :, lo:lo + width] = out.astype(bf16)
        result(b).start()

    def drain(b):
        for d in range(3):
            left(gather_tables(b, d) + third(b, d) + back_third(b, d) + back_second(b, d))
            left(back_relay(b, d) + back_first(b, d) + back_last(b, d))

    pl.semaphore_wait(barrier, peers)
    for copy in own[0]:
        copy.wait()
    start(mixed([gather_near(0, d) for d in narrow_first]))
    weights = [pltpu.make_async_copy(src, dst, wsem.at[k])
               for k, (src, dst) in enumerate(((w1_hbm.at[0], w1), (w3_hbm.at[0], w3), (w2_hbm.at[0], w2)))]
    for copy in weights:
        copy.start()


    later = (iota((tokens, tokens), 0) < iota((tokens, tokens), 1)).astype(f32).astype(bf16)
    expert = expert_at(iota((n, 1), 0), 0)
    gate_rows = jnp.zeros((n, LANES), f32)
    lane = iota((n, LANES), 1)
    perms = [(expert_at(iota((n, 1), 0), d) == expert_at(iota((1, n), 1), 0)).astype(f32).astype(bf16) for d in (1, 2)]
    for b, (ids, gates) in enumerate(((ids1, gt1), (ids2, gt2))):
        member = jnp.zeros((n, tokens), f32)
        gate = jnp.zeros((n, tokens), f32)
        for j in range(ids.shape[0]):
            hit = ids[j:j + 1, :] == expert
            member = jnp.where(hit, 1.0, member)
            gate = jnp.where(hit, gates[j:j + 1, :], gate)
        before = jnp.dot(member.astype(bf16), later, preferred_element_type=f32)
        table = jnp.where(member > 0.0, before + 1.0, 0.0)
        short = table.astype(bf16)
        for d in range(3):
            vt[d][b] = jnp.dot(perms[d - 1], short, preferred_element_type=f32).astype(bf16) if d else short
            vr[d][b, 0] = vt[d][b, 0:plane, :]
        for k in range(CAP):
            col = jnp.sum(jnp.where(table == k + 1.0, gate, 0.0), axis=1, keepdims=True)
            gate_rows = jnp.where(lane == b * CAP + k, col, gate_rows)
    gs[...] = gate_rows[:, None, :]
    start(mixed([gather_tables(0, d) for d in narrow_first]))
    start(gate_first())
    ga[0] = gs[0:plane]
    for copy in own[1]:
        copy.wait()
    start(mixed([gather_near(1, d) + gather_tables(1, d) for d in narrow_first]))
    both(gather_rest)
    both(pick_rows)
    both(last_hop)
    for copy in weights:
        copy.wait()
    both(experts)
    both(lambda b: [left(gather_near(b, d) + gather_relay(b, d)) for d in range(3)])
    tables(0)
    both(return_second)
    both(return_first)
    both(pass_on)
    both(finish)
    left(gate_first() + gate_second() + gate_third())
    both(drain)
    for b in range(2):
        result(b).wait()


def copy_kernel(y, y1, y2, buf, sem):
    pieces = buf.shape[0] // 2
    size = buf.shape[1]
    moves = []
    for k in range(pieces):
        for b, dst in enumerate((y1, y2)):
            slot = 2 * k + b
            part = pl.ds(k * size, size)
            moves.append((pltpu.make_async_copy(y.at[b, part], buf.at[slot], sem.at[0, slot]),
                          pltpu.make_async_copy(buf.at[slot], dst.at[part], sem.at[1, slot])))
    for come, _ in moves:
        come.start()
    for come, go in moves:
        come.wait()
        go.start()
    for _, go in moves:
        go.wait()


def hand_on(y, pieces=4):
    hbm = pl.BlockSpec(memory_space=pl.ANY)
    _, tokens, hidden = y.shape
    shape = jax.ShapeDtypeStruct((tokens, hidden), jnp.bfloat16)
    if tokens // pieces % 16:
        pieces = 1
    return pl.pallas_call(
        copy_kernel, out_shape=(shape, shape), in_specs=[hbm], out_specs=(hbm, hbm),
        scratch_shapes=[pltpu.VMEM((2 * pieces, tokens // pieces, hidden), y.dtype),
                        pltpu.SemaphoreType.DMA((2, 2 * pieces))])(y)


def solution(mesh):
    n_grp = mesh.shape['grp']
    side = round(n_grp ** (1 / 3))
    n = side ** 3 * 2
    plane = n // side
    tok_spec = P(('dp', 'grp', 'ing'), None)
    w_spec = P(('grp', 'ing'), None, None)

    def body(x1, ids1, g1, x2, ids2, g2, w1, w3, w2):
        tokens, hidden = x1.shape
        ff = w1.shape[2]
        vmem = pl.BlockSpec(memory_space=pltpu.VMEM)
        hbm = pl.BlockSpec(memory_space=pl.ANY)
        out = jax.ShapeDtypeStruct((2, tokens, hidden), jnp.bfloat16)
        widths = [w for _, w in lane_parts(hidden)]

        def per_part(*shape):
            return [pltpu.VMEM((*shape, w), jnp.bfloat16) for w in widths]

        def wide(*shape):
            return [pltpu.VMEM((*shape, w), jnp.float32) for w in widths]

        def per_dim(*shape):
            return [pltpu.VMEM(shape, jnp.bfloat16) for _ in widths]

        rows = plane * CAP

        def gate(*shape):
            return pltpu.VMEM((*shape, 1, LANES), jnp.float32)

        y = pl.pallas_call(
            functools.partial(moe_kernel, side),
            out_shape=out,
            in_specs=[hbm] * 2 + [vmem] * 4 + [hbm] * 3,
            out_specs=hbm,
            scratch_shapes=[per_part(2, side, tokens),
                            per_part(2, side, side, 2, side, CAP),
                            per_part(2, side, 2, side, side, CAP),
                            [pltpu.VMEM((2, side, *((side, side, 2) if d < 2 else (side, 2, side)), CAP, w), jnp.bfloat16)
                             for d, w in enumerate(widths)],
                            wide(2, side - 1, tokens), wide(2, 2, tokens), wide(2, 2, tokens // 2),
                            per_dim(2, n, tokens),
                            per_dim(2, side, plane, tokens),
                            pltpu.VMEM((2, side, side, side, 2, CAP, hidden), jnp.bfloat16),
                            gate(n), gate(side, plane), gate(side, side, 2 * side), gate(side, side, 2 * side),
                            pltpu.VMEM((hidden, ff), jnp.bfloat16),
                            pltpu.VMEM((hidden, ff), jnp.bfloat16),
                            pltpu.VMEM((ff, hidden), jnp.bfloat16),
                            pltpu.VMEM((2, tokens, hidden), jnp.float32),
                            pltpu.VMEM((2, tokens, hidden), jnp.bfloat16),
                            pltpu.SemaphoreType.DMA((2, 3)), pltpu.SemaphoreType.DMA((2,)),
                            pltpu.SemaphoreType.DMA((3,)), pltpu.SemaphoreType.DMA((2, 3, 2 * side)),
                            [pltpu.SemaphoreType.DMA((2, 2, 3, k * side)) for k in (1, 1, 1, 2, 2, 1, 3)]],
            compiler_params=pltpu.CompilerParams(collective_id=0, has_side_effects=True,
                                                 vmem_limit_bytes=67_000_000),
        )(x1, x2, ids1.T, ids2.T, g1.T, g2.T, w1, w3, w2)
        return hand_on(y)

    return jax.shard_map(body, mesh=mesh, in_specs=(tok_spec,) * 6 + (w_spec,) * 3,
                         out_specs=(tok_spec, tok_spec), check_vma=False)
```

time: 185 us -> 183 us (0.989)
  Pallas kernels: 184 us -> 182 us
    pallas_call x1, Pallas kernels: 182 us -> 180 us  [body(): pl.pallas_call(functools.partial(moe_kernel, side), out_shape=out, in_spe...]
where the time goes in v4:
time: 183 us
  Pallas kernels  182 us (99%)
    pallas_call x1, Pallas kernels, body(): pl.pallas_call(functools.partial(moe_kernel, side), out_shape=out, in_spe...  180 us

profile of v4, /device:TPU:1, one launch (start us, length us, event | category | flops | bytes accessed | tf_op | source)
XLA Modules:
  0.0 182.6 jit_solution(12256663984359700253)
XLA Ops:
  0.6 179.8 %shard_map.104.y = bf16[2,128,2048]{2,1,0:T(8,128)(2,1)} custom-call(bf16[128,2048]{1,0:T(8,128)(2,1)} %x1.1, bf16[128,2048]{1,0:T(8,128)(2,1)} %x2.1, s32[8,128]{1,0:T(8,128)} %bitcast.4, s32[8,128]{1,0:T(8,128)} %bitcast.5, f32[8,128]{1,0:T(8,128)} %bitcast.6, f32[8,128]{1,0:T(8,128)} %bitcast.7, bf16[1,2048,768]{2,1,0:T(8,128)(2,1)} %w1_hbm.1, ...), custom_call_target="tpu_custom_call" | custom-call | tf_op jit(solution)/shard_map/pallas_call | solution.py:449
  180.5 2.1 %shard_map.105 = (bf16[128,2048]{1,0:T(8,128)(2,1)}, bf16[128,2048]{1,0:T(8,128)(2,1)}) custom-call(bf16[2,128,2048]{2,1,0:T(8,128)(2,1)} %shard_map.104.y), custom_call_target="tpu_custom_call" | custom-call | tf_op jit(solution)/shard_map/pallas_call | solution.py:413

commit v5 on v4

--- a/solution.py
+++ b/solution.py
@@ -73,8 +73,8 @@
         return to_grp * 2 + to_ing
 
     up = [f < s for f, s, t in order]
-    every = range(1, side)
-    ends = [(k, c) for k in range(side) for c in range(2) if k + c]
+    every = sorted(range(1, side), key=lambda k: k == side // 2 and side > 2)
+    ends = [(0, 1)] + [(k, c) for k in every for c in range(2)]
 
     def sem(phase, b, d, k):
         return sems[phase].at[0, b, d, k], sems[phase].at[1, b, d, k]
@@ -111,9 +111,12 @@
         return [remote(p2r[d].at[b, k, c], xr.at[final(d, b, k, c)], *sem(3, b, d, 2 * k + c), along(order[d][2], k, c))
                 for k, c in ends]
 
+    def back_one(b, d, k, c):
+        return remote(xr.at[final(d, b, k, c)], p2s[d].at[b, :, k, c], *sem(4, b, d, 2 * k + c),
+                      along(order[d][2], -k, c))
+
     def back_third(b, d):
-        return [remote(xr.at[final(d, b, k, c)], p2s[d].at[b, :, k, c], *sem(4, b, d, 2 * k + c),
-                       along(order[d][2], -k, c)) for k, c in ends]
+        return [back_one(b, d, k, c) for k, c in ends]
 
     def back_mid(d, b, j):
         return (b, slice(None), slice(None), slice(None), j) if up[d] else (b, j)
@@ -209,6 +212,8 @@
             g = jnp.sum(jnp.where(mine, g, 0.0), axis=1, keepdims=True)
             out = jnp.dot(inner, w2[...], preferred_element_type=f32) * g
             xr[b, ox] = out.reshape(side, side, 2, CAP, hidden).astype(bf16)
+            for c in range(2):
+                pl.when(ox + c > 0)(back_one(b, 1, ox, c).start)
             return carry
 
         lax.fori_loop(0, side, chunk, 0)
@@ -267,7 +272,8 @@
         for d in narrow_first:
             arrived(second(b, d))
             left(second(b, d))
-            start(third(b, d))
+        start(mixed([third(b, d) for d in narrow_first]))
+        for d in narrow_first:
             xr[final(d, b, 0, 0)] = p2r[d][b, 0, 0]
 
         @pl.when(b == 0)
@@ -281,14 +287,15 @@
             arrived(third(b, d))
         pl.when(b == 0)(lambda: arrived(gate_third()))
         ffn(b)
-        start(mixed([back_third(b, d) for d in narrow_first]))
+        start(mixed([back_third(b, d) for d in (2, 0)]))
         for d in narrow_first:
             p2s[d][b, :, 0, 0] = xr[final(d, b, 0, 0)]
 
     def return_second(b):
         for d in narrow_first:
             arrived(back_third(b, d))
-            start(back_second(b, d))
+        start(mixed([back_second(b, d) for d in narrow_first]))
+        for d in narrow_first:
             r2[d][b, 0] = p2s[d][back_mid(d, b, 0)]
 
     def return_first(b):

time: 183 us -> 182 us (level)
  no operation moved by 1% of the time
where the time goes in v5:
time: 182 us
  Pallas kernels  181 us (99%)
    pallas_call x1, Pallas kernels, body(): pl.pallas_call(functools.partial(moe_kernel, side), out_shape=out, in_spe...  179 us

profile of v5, /device:TPU:1, one launch (start us, length us, event | category | flops | bytes accessed | tf_op | source)
XLA Modules:
  0.0 181.7 jit_solution(14599427821739247498)
XLA Ops:
  0.6 178.9 %shard_map.104.y = bf16[2,128,2048]{2,1,0:T(8,128)(2,1)} custom-call(bf16[128,2048]{1,0:T(8,128)(2,1)} %x1.1, bf16[128,2048]{1,0:T(8,128)(2,1)} %x2.1, s32[8,128]{1,0:T(8,128)} %bitcast.4, s32[8,128]{1,0:T(8,128)} %bitcast.5, f32[8,128]{1,0:T(8,128)} %bitcast.6, f32[8,128]{1,0:T(8,128)} %bitcast.7, bf16[1,2048,768]{2,1,0:T(8,128)(2,1)} %w1_hbm.1, ...), custom_call_target="tpu_custom_call" | custom-call | tf_op jit(solution)/shard_map/pallas_call | solution.py:456
  179.6 2.1 %shard_map.105 = (bf16[128,2048]{1,0:T(8,128)(2,1)}, bf16[128,2048]{1,0:T(8,128)(2,1)}) custom-call(bf16[2,128,2048]{2,1,0:T(8,128)(2,1)} %shard_map.104.y), custom_call_target="tpu_custom_call" | custom-call | tf_op jit(solution)/shard_map/pallas_call | solution.py:420

commit v6 on v5

--- a/solution.py
+++ b/solution.py
@@ -18,9 +18,9 @@
     return [(sum(sizes[:d]), sizes[d]) for d in range(3)]
 
 
-def moe_kernel(side, x1, x2, ids1, ids2, gt1, gt2, w1_hbm, w3_hbm, w2_hbm, y,
-               ag, p2s, p2r, r2, ps, pr, rel, vt, vr, xr, gs, ga, gb, gr, w1, w3, w2, total, rounded,
-               xsem, ysem, wsem, gsem, sems):
+def moe_kernel(side, x1, x2, ids1_hbm, ids2_hbm, gt1_hbm, gt2_hbm, w1_hbm, w3_hbm, w2_hbm, y,
+               ag, p2s, p2r, r2, ps, pr, rel, vt, vr, xr, gs, ga, gb, gr, w1, w3, w2, total, rounded, ids1, ids2, gt1, gt2,
+               rsem, xsem, ysem, wsem, gsem, sems):
     xs = (x1, x2)
     tokens, hidden = x1.shape
     n = side ** 3 * 2
@@ -61,9 +61,11 @@
 
         lax.fori_loop(2 if dim else 1, 2 * side, knock, 0)
     peers = 6 * side - 5
+    routes = [pltpu.make_async_copy(src, dst, rsem.at[k]) for k, (src, dst) in enumerate(
+        ((ids1_hbm, ids1), (ids2_hbm, ids2), (gt1_hbm, gt1), (gt2_hbm, gt2)))]
     own = [[pltpu.make_async_copy(xs[b].at[:, pl.ds(lo, width)], ag[d].at[b, 0], xsem.at[b, d])
             for d, (lo, width) in enumerate(parts)] for b in range(2)]
-    for copy in own[0] + own[1]:
+    for copy in own[0] + routes + own[1]:
         copy.start()
     def expert_at(q, d):
         off = [None] * 3
@@ -183,10 +185,11 @@
         v = jnp.dot(expand(), table, preferred_element_type=f32)
         return jnp.where(v == (iota(v.shape, 0) % CAP + 1).astype(f32), 1.0, 0.0)
 
-    def select(b, d):
+    def select(b, d, first, last):
         width = parts[d][1]
 
-        def pick(i, carry):
+        def pick(m, carry):
+            i = (m + side - 1) % side
             sel = chosen(vr[d][b, i]).astype(bf16)
             out = jnp.dot(sel, ag[d][b, i], preferred_element_type=f32)
             out = out.reshape(side, side, 2, CAP, width).astype(bf16)
@@ -198,7 +201,7 @@
                 p2s[d][b, j, :, :, i] = out[j]
             return carry
 
-        lax.fori_loop(0, side, pick, 0)
+        lax.fori_loop(first, last, pick, 0)
 
     def ffn(b):
         def chunk(ox, carry):
@@ -255,11 +258,14 @@
         for d in narrow_first:
             arrived(gather_near(b, d))
             start(gather_relay(b, d))
+        for d in narrow_first:
+            arrived(gather_tables(b, d))
+            select(b, d, 0, side - 1)
 
     def pick_rows(b):
         for d in narrow_first:
-            arrived(gather_tables(b, d) + gather_relay(b, d))
-            select(b, d)
+            arrived(gather_relay(b, d))
+            select(b, d, side - 1, side)
             start(second(b, d))
 
         @pl.when(b == 0)
@@ -345,6 +351,9 @@
     for copy in weights:
         copy.start()
 
+
+    for copy in routes:
+        copy.wait()
 
     later = (iota((tokens, tokens), 0) < iota((tokens, tokens), 1)).astype(f32).astype(bf16)
     expert = expert_at(iota((n, 1), 0), 0)
@@ -411,7 +420,7 @@
         go.wait()
 
 
-def hand_on(y, pieces=4):
+def hand_on(y, pieces=2):
     hbm = pl.BlockSpec(memory_space=pl.ANY)
     _, tokens, hidden = y.shape
     shape = jax.ShapeDtypeStruct((tokens, hidden), jnp.bfloat16)
@@ -434,7 +443,7 @@
     def body(x1, ids1, g1, x2, ids2, g2, w1, w3, w2):
         tokens, hidden = x1.shape
         ff = w1.shape[2]
-        vmem = pl.BlockSpec(memory_space=pltpu.VMEM)
+        top_k = ids1.shape[1]
         hbm = pl.BlockSpec(memory_space=pl.ANY)
         out = jax.ShapeDtypeStruct((2, tokens, hidden), jnp.bfloat16)
         widths = [w for _, w in lane_parts(hidden)]
@@ -456,7 +465,7 @@
         y = pl.pallas_call(
             functools.partial(moe_kernel, side),
             out_shape=out,
-            in_specs=[hbm] * 2 + [vmem] * 4 + [hbm] * 3,
+            in_specs=[hbm] * 9,
             out_specs=hbm,
             scratch_shapes=[per_part(2, side, tokens),
                             per_part(2, side, side, 2, side, CAP),
@@ -473,7 +482,8 @@
                             pltpu.VMEM((ff, hidden), jnp.bfloat16),
                             pltpu.VMEM((2, tokens, hidden), jnp.float32),
                             pltpu.VMEM((2, tokens, hidden), jnp.bfloat16),
-                            pltpu.SemaphoreType.DMA((2, 3)), pltpu.SemaphoreType.DMA((2,)),
+                            *[pltpu.VMEM((top_k, tokens), t) for t in (ids1.dtype, ids2.dtype, g1.dtype, g2.dtype)],
+                            pltpu.SemaphoreType.DMA((4,)), pltpu.SemaphoreType.DMA((2, 3)), pltpu.SemaphoreType.DMA((2,)),
                             pltpu.SemaphoreType.DMA((3,)), pltpu.SemaphoreType.DMA((2, 3, 2 * side)),
                             [pltpu.SemaphoreType.DMA((2, 2, 3, k * side)) for k in (1, 1, 1, 2, 2, 1, 3)]],
             compiler_params=pltpu.CompilerParams(collective_id=0, has_side_effects=True,

time: 182 us -> 181 us (level)
  no operation moved by 1% of the time
where the time goes in v6:
time: 181 us
  Pallas kernels  181 us (100%)
    pallas_call x1, Pallas kernels, body(): pl.pallas_call(functools.partial(moe_kernel, side), out_shape=out, in_spe...  179 us

profile of v6, /device:TPU:1, one launch (start us, length us, event | category | flops | bytes accessed | tf_op | source)
XLA Modules:
  0.0 181.4 jit_solution(18071540168269384941)
XLA Ops:
  0.6 178.7 %shard_map.104.y = bf16[2,128,2048]{2,1,0:T(8,128)(2,1)} custom-call(bf16[128,2048]{1,0:T(8,128)(2,1)} %x1.1, bf16[128,2048]{1,0:T(8,128)(2,1)} %x2.1, s32[8,128]{1,0:T(8,128)} %bitcast.4, s32[8,128]{1,0:T(8,128)} %bitcast.5, f32[8,128]{1,0:T(8,128)} %bitcast.6, f32[8,128]{1,0:T(8,128)} %bitcast.7, bf16[1,2048,768]{2,1,0:T(8,128)(2,1)} %w1_hbm.1, ...), custom_call_target="tpu_custom_call" | custom-call | tf_op jit(solution)/shard_map/pallas_call | solution.py:465
  179.4 2.0 %shard_map.105 = (bf16[128,2048]{1,0:T(8,128)(2,1)}, bf16[128,2048]{1,0:T(8,128)(2,1)}) custom-call(bf16[2,128,2048]{2,1,0:T(8,128)(2,1)} %shard_map.104.y), custom_call_target="tpu_custom_call" | custom-call | tf_op jit(solution)/shard_map/pallas_call | solution.py:429

commit v7 on v6

--- a/solution.py
+++ b/solution.py
@@ -113,12 +113,20 @@
         return [remote(p2r[d].at[b, k, c], xr.at[final(d, b, k, c)], *sem(3, b, d, 2 * k + c), along(order[d][2], k, c))
                 for k, c in ends]
 
-    def back_one(b, d, k, c):
-        return remote(xr.at[final(d, b, k, c)], p2s[d].at[b, :, k, c], *sem(4, b, d, 2 * k + c),
-                      along(order[d][2], -k, c))
+    piece = side // 2
+
+    def back_one(b, d, k, c, h):
+        if d == 1:
+            src, dst = final(d, b, k, c), (b, slice(None), k, c)
+        else:
+            part = pl.ds(h * piece, piece)
+            src = list(final(d, b, k, c))
+            src[1] = part
+            src, dst = tuple(src), (b, part, k, c)
+        return remote(xr.at[src], p2s[d].at[dst], *sem(4, b, d, (2 * k + c) * 2 + h), along(order[d][2], -k, c))
 
     def back_third(b, d):
-        return [back_one(b, d, k, c) for k, c in ends]
+        return [back_one(b, d, k, c, h) for h in range(1 if d == 1 else 2) for k, c in ends]
 
     def back_mid(d, b, j):
         return (b, slice(None), slice(None), slice(None), j) if up[d] else (b, j)
@@ -216,7 +224,12 @@
             out = jnp.dot(inner, w2[...], preferred_element_type=f32) * g
             xr[b, ox] = out.reshape(side, side, 2, CAP, hidden).astype(bf16)
             for c in range(2):
-                pl.when(ox + c > 0)(back_one(b, 1, ox, c).start)
+                pl.when(ox + c > 0)(back_one(b, 1, ox, c, 0).start)
+
+            @pl.when(ox % piece == piece - 1)
+            def _():
+                start(mixed([[back_one(b, d, k, c, ox // piece) for k, c in ends] for d in (2, 0)]))
+
             return carry
 
         lax.fori_loop(0, side, chunk, 0)
@@ -293,7 +306,6 @@
             arrived(third(b, d))
         pl.when(b == 0)(lambda: arrived(gate_third()))
         ffn(b)
-        start(mixed([back_third(b, d) for d in (2, 0)]))
         for d in narrow_first:
             p2s[d][b, :, 0, 0] = xr[final(d, b, 0, 0)]
 
@@ -485,7 +497,7 @@
                             *[pltpu.VMEM((top_k, tokens), t) for t in (ids1.dtype, ids2.dtype, g1.dtype, g2.dtype)],
                             pltpu.SemaphoreType.DMA((4,)), pltpu.SemaphoreType.DMA((2, 3)), pltpu.SemaphoreType.DMA((2,)),
                             pltpu.SemaphoreType.DMA((3,)), pltpu.SemaphoreType.DMA((2, 3, 2 * side)),
-                            [pltpu.SemaphoreType.DMA((2, 2, 3, k * side)) for k in (1, 1, 1, 2, 2, 1, 3)]],
+                            [pltpu.SemaphoreType.DMA((2, 2, 3, k * side)) for k in (1, 1, 1, 2, 4, 1, 3)]],
             compiler_params=pltpu.CompilerParams(collective_id=0, has_side_effects=True,
                                                  vmem_limit_bytes=67_000_000),
         )(x1, x2, ids1.T, ids2.T, g1.T, g2.T, w1, w3, w2)

time: 181 us -> 182 us (level)
  no operation moved by 1% of the time
where the time goes in v7:
time: 182 us
  Pallas kernels  181 us (99%)
    pallas_call x1, Pallas kernels, body(): pl.pallas_call(functools.partial(moe_kernel, side), out_shape=out, in_spe...  179 us

profile of v7, /device:TPU:1, one launch (start us, length us, event | category | flops | bytes accessed | tf_op | source)
XLA Modules:
  0.0 181.7 jit_solution(17305695176864067515)
XLA Ops:
  0.6 179.1 %shard_map.104.y = bf16[2,128,2048]{2,1,0:T(8,128)(2,1)} custom-call(bf16[128,2048]{1,0:T(8,128)(2,1)} %x1.1, bf16[128,2048]{1,0:T(8,128)(2,1)} %x2.1, s32[8,128]{1,0:T(8,128)} %bitcast.4, s32[8,128]{1,0:T(8,128)} %bitcast.5, f32[8,128]{1,0:T(8,128)} %bitcast.6, f32[8,128]{1,0:T(8,128)} %bitcast.7, bf16[1,2048,768]{2,1,0:T(8,128)(2,1)} %w1_hbm.1, ...), custom_call_target="tpu_custom_call" | custom-call | tf_op jit(solution)/shard_map/pallas_call | solution.py:477
  179.8 2.0 %shard_map.105 = (bf16[128,2048]{1,0:T(8,128)(2,1)}, bf16[128,2048]{1,0:T(8,128)(2,1)}) custom-call(bf16[2,128,2048]{2,1,0:T(8,128)(2,1)} %shard_map.104.y), custom_call_target="tpu_custom_call" | custom-call | tf_op jit(solution)/shard_map/pallas_call | solution.py:441

commit v8 on v6

--- a/solution.py
+++ b/solution.py
@@ -245,7 +245,7 @@
         part = jnp.dot(fold, z, preferred_element_type=f32).astype(bf16)
         return jnp.dot(ag[d][1, i, :, 0:rows], part, preferred_element_type=f32)
 
-    narrow_first = (1, 2, 0)
+    narrow_first, wide_first = (1, 2, 0), (0, 1, 2)
 
     def both(body):
         def step(b, carry):
@@ -305,7 +305,7 @@
             r2[d][b, 0] = p2s[d][back_mid(d, b, 0)]
 
     def return_first(b):
-        for d, (lo, width) in [(d, parts[d]) for d in narrow_first]:
+        for d, (lo, width) in [(d, parts[d]) for d in wide_first]:
             arrived(back_second(b, d))
 
             def one(i, carry, d=d):
@@ -319,7 +319,7 @@
 
     def pass_on(b):
         half = tokens // 2
-        for d in narrow_first:
+        for d in wide_first:
             arrived(back_relay(b, d))
             if ring:
                 ps[d][b, 0, 0:half] += rel[d][b, 0]
@@ -330,7 +330,7 @@
         return pltpu.make_async_copy(rounded.at[b], y.at[b], ysem.at[b])
 
     def finish(b):
-        for d, (lo, width) in [(d, parts[d]) for d in narrow_first]:
+        for d, (lo, width) in [(d, parts[d]) for d in wide_first]:
             arrived(back_first(b, d) + back_last(b, d))
             out = total[b, :, lo:lo + width] + pr[d][b, 0]
             out = out + pr[d][b, 1] if ring else out

time: 181 us -> 181 us (level)
  no operation moved by 1% of the time
where the time goes in v8:
time: 181 us
  Pallas kernels  181 us (100%)
    pallas_call x1, Pallas kernels, body(): pl.pallas_call(functools.partial(moe_kernel, side), out_shape=out, in_spe...  179 us

profile of v8, /device:TPU:1, one launch (start us, length us, event | category | flops | bytes accessed | tf_op | source)
XLA Modules:
  0.0 181.3 jit_solution(3369403113352702814)
XLA Ops:
  0.6 178.7 %shard_map.104.y = bf16[2,128,2048]{2,1,0:T(8,128)(2,1)} custom-call(bf16[128,2048]{1,0:T(8,128)(2,1)} %x1.1, bf16[128,2048]{1,0:T(8,128)(2,1)} %x2.1, s32[8,128]{1,0:T(8,128)} %bitcast.4, s32[8,128]{1,0:T(8,128)} %bitcast.5, f32[8,128]{1,0:T(8,128)} %bitcast.6, f32[8,128]{1,0:T(8,128)} %bitcast.7, bf16[1,2048,768]{2,1,0:T(8,128)(2,1)} %w1_hbm.1, ...), custom_call_target="tpu_custom_call" | custom-call | tf_op jit(solution)/shard_map/pallas_call | solution.py:465
  179.3 2.0 %shard_map.105 = (bf16[128,2048]{1,0:T(8,128)(2,1)}, bf16[128,2048]{1,0:T(8,128)(2,1)}) custom-call(bf16[2,128,2048]{2,1,0:T(8,128)(2,1)} %shard_map.104.y), custom_call_target="tpu_custom_call" | custom-call | tf_op jit(solution)/shard_map/pallas_call | solution.py:429

commit v9 on v8

--- a/solution.py
+++ b/solution.py
@@ -245,7 +245,7 @@
         part = jnp.dot(fold, z, preferred_element_type=f32).astype(bf16)
         return jnp.dot(ag[d][1, i, :, 0:rows], part, preferred_element_type=f32)
 
-    narrow_first, wide_first = (1, 2, 0), (0, 1, 2)
+    narrow_first, wide_first = (0, 1, 2), (0, 1, 2)
 
     def both(body):
         def step(b, carry):

time: 181 us -> 181 us (level)
  no operation moved by 1% of the time
where the time goes in v9:
time: 181 us
  Pallas kernels  180 us (99%)
    pallas_call x1, Pallas kernels, body(): pl.pallas_call(functools.partial(moe_kernel, side), out_shape=out, in_spe...  178 us

profile of v9, /device:TPU:1, one launch (start us, length us, event | category | flops | bytes accessed | tf_op | source)
XLA Modules:
  0.0 180.9 jit_solution(1147714955281553863)
XLA Ops:
  0.6 178.3 %shard_map.104.y = bf16[2,128,2048]{2,1,0:T(8,128)(2,1)} custom-call(bf16[128,2048]{1,0:T(8,128)(2,1)} %x1.1, bf16[128,2048]{1,0:T(8,128)(2,1)} %x2.1, s32[8,128]{1,0:T(8,128)} %bitcast.4, s32[8,128]{1,0:T(8,128)} %bitcast.5, f32[8,128]{1,0:T(8,128)} %bitcast.6, f32[8,128]{1,0:T(8,128)} %bitcast.7, bf16[1,2048,768]{2,1,0:T(8,128)(2,1)} %w1_hbm.1, ...), custom_call_target="tpu_custom_call" | custom-call | tf_op jit(solution)/shard_map/pallas_call | solution.py:465
  178.9 2.0 %shard_map.105 = (bf16[128,2048]{1,0:T(8,128)(2,1)}, bf16[128,2048]{1,0:T(8,128)(2,1)}) custom-call(bf16[2,128,2048]{2,1,0:T(8,128)(2,1)} %shard_map.104.y), custom_call_target="tpu_custom_call" | custom-call | tf_op jit(solution)/shard_map/pallas_call | solution.py:429
